TPU v7x, 256 devices: a whole 4x4x8 slice. The times are simulated.
256 devices in a mesh: gx: 8 (over z), gy: 8 (over y, core), gz: 4 (over x).
Axes of the slice: x: 4, y: 4, z: 8, core: 2. Of those that a mesh axis runs over, the one named last changes fastest.
Arguments:
- positions: float32 [3, 16, 16, 32, 128], P(None, 'gx', 'gy', 'gz'), may hold values from 0 to 1
- shield: float32 [16, 16, 32, 128], P('gx', 'gy', 'gz'), may hold values from 0.3 to 1
- width: float32 [16, 16, 32, 128], P('gx', 'gy', 'gz'), may hold values from 0.5 to 2
- hardness: float32 [16, 16, 32, 128], P('gx', 'gy', 'gz'), may hold values from 0.5 to 2
- softness: float32 [16, 16, 32, 128], P('gx', 'gy', 'gz'), may hold values from 0.5 to 2
- coupling: float32 [16, 16, 32, 128], P('gx', 'gy', 'gz'), may hold values from -0.45 to 0.45
- pair_bits: int32 [16, 16, 32], P('gx', 'gy', 'gz'), may hold values from 8192 to 134217727
- right_side: float32 [4, 16, 16, 32, 128], P(None, 'gx', 'gy', 'gz'), may hold values from -7 to 7
Outputs:
- solution: float32 [4, 16, 16, 32, 128], P(None, 'gx', 'gy', 'gz')
- residual: float32 [4, 16, 16, 32, 128], P(None, 'gx', 'gy', 'gz')
All inputs are finite; a program needn't handle non-finite values.
Results may differ from a plain program's by a relative error of at most 0.0018.
Values sent between devices are 32-bit elements; how exact they have to be, the bound alone decides.
A program may use at most 128 MiB of HBM per device.

v0:
```python
import functools

import jax
import jax.numpy as jnp
from jax import lax
from jax.sharding import Mesh
from jax.sharding import PartitionSpec as P

ITERS = 3
GX_GY_GZ = ("gx", "gy_0", "gy_1", "gz")
GY = ("gy_0", "gy_1")


coulomb_scale = 0.002
response_scale = 0.003


def extended(block, sides, width):
    for axis, dim in sides:
        count = lax.axis_size(axis)
        forward = [(i, i + 1) for i in range(count - 1)]
        backward = [(target, source) for source, target in forward]
        low = lax.ppermute(
            lax.slice_in_dim(block, block.shape[dim] - width, None, axis=dim), axis, forward
        )
        high = lax.ppermute(lax.slice_in_dim(block, 0, width, axis=dim), axis, backward)
        block = jnp.concatenate([low, block, high], axis=dim)
    return block


def one_axis_at_a_time(shard, axes):
    return functools.reduce(lax.psum, axes, shard)


def index_tuple(values):
    return tuple((jnp.asarray(value).astype(jnp.int32) for value in values))


def pair_terms(own_params, partner, offset_code, own_bits):
    shift_first = (offset_code // 9 - 1).astype(jnp.float32)
    shift_second = (offset_code // 3 % 3 - 1).astype(jnp.float32)
    shift_third = (offset_code % 3 - 1).astype(jnp.float32)

    def separation(column, shift):
        return shift + (partner[column][:, None, :] - own_params[column][:, :, None])

    first = separation(0, shift_first)
    second = separation(1, shift_second)
    third = separation(2, shift_third)
    distance = first * first + second * second + third * third
    coulomb = coulomb_scale * lax.rsqrt(
        distance + own_params[3][:, :, None] * partner[3][:, None, :]
    )
    response = response_scale * jnp.exp(
        -distance / (own_params[4][:, :, None] + partner[4][:, None, :])
    )
    listed = jnp.right_shift(own_bits, offset_code) & 1 > 0
    tile_size = own_params.shape[2]
    diagonal_mask = lax.broadcasted_iota(
        jnp.int32, (tile_size, tile_size), 0
    ) == lax.broadcasted_iota(jnp.int32, (tile_size, tile_size), 1)
    kept = listed[:, None, None] & jnp.logical_not(diagonal_mask[None] & (offset_code == 13))
    empty_pair = jnp.zeros_like(distance)
    return (
        jnp.where(kept, coulomb, empty_pair).astype(jnp.bfloat16),
        jnp.where(kept, response, empty_pair).astype(jnp.bfloat16),
    )


def tile_block(padded, offset_code, extent):
    fields = padded.shape[0]
    tile_size = padded.shape[4]
    start = index_tuple((0, offset_code // 9, offset_code // 3 % 3, offset_code % 3, 0))
    block = lax.dynamic_slice(padded, start, (fields, extent[0], extent[1], extent[2], tile_size))
    return block.reshape(fields, extent[0] * extent[1] * extent[2], tile_size)


def static_block(padded, offset_code, extent):
    first = offset_code // 9
    second = offset_code // 3 % 3
    third = offset_code % 3
    block = padded[
        :, first : first + extent[0], second : second + extent[1], third : third + extent[2]
    ]
    return block.reshape(padded.shape[0], extent[0] * extent[1] * extent[2], padded.shape[4])


def spread_ghosts(vector, extent):
    shaped = vector.reshape(4, extent[0], extent[1], extent[2], vector.shape[2])
    return extended(shaped, (("gx", 1), (GY, 2), ("gz", 3)), 1)


def split_parts(padded):
    upper = padded.astype(jnp.bfloat16)
    lower = (padded - upper.astype(jnp.float32)).astype(jnp.bfloat16)
    return jnp.concatenate([upper[:2], lower[:2], upper[2:], lower[2:]], axis=0)


def inner_local(vector, other_vector):
    return jnp.sum((vector * other_vector).reshape(2, 2, -1), axis=(0, 2))


def two_products(vector, applied):
    return (
        one_axis_at_a_time(inner_local(vector, vector), GX_GY_GZ),
        one_axis_at_a_time(inner_local(vector, applied), GX_GY_GZ),
    )


def widen(scalars):
    return jnp.concatenate([scalars, scalars]).reshape(4, 1, 1)


def on_device(positions, shield, width, hardness, softness, coupling, pair_bits, right_side):
    tiles_x, tiles_y, tiles_z, tile_size = hardness.shape
    extent = (tiles_x, tiles_y, tiles_z)
    tile_count = tiles_x * tiles_y * tiles_z
    params = jnp.concatenate([positions, shield[None], width[None]], axis=0)
    joined = extended(
        jnp.concatenate([params, right_side], axis=0), (("gx", 1), (GY, 2), ("gz", 3)), 1
    )
    params_pad = joined[:5]
    first_pad = joined[5:]
    own_params = params_pad[:, 1:-1, 1:-1, 1:-1].reshape(5, tile_count, tile_size)
    own_bits = pair_bits.reshape(tile_count)

    def build(offset_code, carry):
        store_coulomb, store_response, row_coulomb, row_response = carry
        offset_code = offset_code.astype(jnp.int32)
        partner = tile_block(params_pad, offset_code, extent)
        coulomb, response = pair_terms(own_params, partner, offset_code, own_bits)
        store_coulomb = lax.dynamic_update_index_in_dim(store_coulomb, coulomb, offset_code, 0)
        store_response = lax.dynamic_update_index_in_dim(store_response, response, offset_code, 0)
        row_coulomb = row_coulomb + jnp.sum(coulomb.astype(jnp.float32), axis=2)
        row_response = row_response + jnp.sum(response.astype(jnp.float32), axis=2)
        return (store_coulomb, store_response, row_coulomb, row_response)

    store_zeros = jnp.zeros((27, tile_count, tile_size, tile_size), jnp.bfloat16)
    flat_zeros = jnp.zeros((tile_count, tile_size), jnp.float32)
    store_coulomb, store_response, row_coulomb, row_response = lax.fori_loop(
        0, 27, build, (store_zeros, store_zeros, flat_zeros, flat_zeros)
    )
    diagonal_charge = hardness.reshape(tile_count, tile_size) + row_coulomb
    diagonal_potential = softness.reshape(tile_count, tile_size) + row_response
    linking = coupling.reshape(tile_count, tile_size)

    def operate(padded, vector):
        parts_pad = split_parts(padded)
        stacked = jnp.stack(
            [static_block(parts_pad, offset_code, extent) for offset_code in range(27)], axis=0
        )
        charge_terms = jnp.einsum(
            "otij,oftj->fti", store_coulomb, stacked[:, :4], preferred_element_type=jnp.float32
        )
        potential_terms = jnp.einsum(
            "otij,oftj->fti", store_response, stacked[:, 4:], preferred_element_type=jnp.float32
        )
        pair_charge = charge_terms[:2] + charge_terms[2:]
        pair_potential = potential_terms[:2] + potential_terms[2:]
        image_charge = diagonal_charge * vector[:2] + pair_charge + linking * vector[2:]
        image_potential = diagonal_potential * vector[2:] - pair_potential + linking * vector[:2]
        return jnp.concatenate([image_charge, image_potential], axis=0)

    rhs_flat = right_side.reshape(4, tile_count, tile_size)
    solution = jnp.zeros_like(rhs_flat)
    applied = operate(first_pad, rhs_flat)
    norm_now, product = two_products(rhs_flat, applied)
    step_size = norm_now / product
    remainder = rhs_flat
    direction = rhs_flat
    along = applied
    for iteration in range(ITERS):
        solution = solution + widen(step_size) * direction
        remainder = remainder - widen(step_size) * along
        if iteration + 1 < ITERS:
            applied = operate(spread_ghosts(remainder, extent), remainder)
            norm_next, product = two_products(remainder, applied)
            beta_ratio = norm_next / norm_now
            step_size = norm_next / (product - beta_ratio * norm_next / step_size)
            direction = remainder + widen(beta_ratio) * direction
            along = applied + widen(beta_ratio) * along
            norm_now = norm_next
    shape_out = (4, tiles_x, tiles_y, tiles_z, tile_size)
    return (solution.reshape(shape_out), remainder.reshape(shape_out))


def solution(mesh):
    finer = Mesh(
        mesh.devices.reshape(mesh.shape["gx"], 4, 2, mesh.shape["gz"]), ("gx", "gy_0", "gy_1", "gz")
    )
    placed = (
        P(None, "gx", GY, "gz", None),
        P("gx", GY, "gz", None),
        P("gx", GY, "gz", None),
        P("gx", GY, "gz", None),
        P("gx", GY, "gz", None),
        P("gx", GY, "gz", None),
        P("gx", GY, "gz"),
        P(None, "gx", GY, "gz", None),
    )
    return jax.shard_map(
        on_device,
        mesh=finer,
        in_specs=placed,
        out_specs=(P(None, "gx", GY, "gz", None), P(None, "gx", GY, "gz", None)),
        check_vma=False,
    )
```

profile of v0, /device:TPU:1, one launch (start us, length us, event | category | flops | bytes accessed | tf_op | source)
XLA Modules:
  0.0 565.8 jit_solution(10181508359719995102)
XLA Ops:
  10.2 5.2 collective-permute-start.3
  29.4 282.6 %while.23 = (s32[]{:T(128)}, bf16[27,32,128,128]{3,2,0,1:T(8,128)(2,1)}, bf16[27,32,128,128]{3,2,0,1:T(8,128)(2,1)}, f32[32,128]{1,0:T(8,128)S(1)}, f32[32,128]{...) while((s32[]{:T(128)}, ...), condition=%wide.region_9.10_spmd.clone, body=%wide.region_6.9_spmd.clone.sunk | while | flops 26271884 | bytes 2933673 | solution.py:140
  29.5 5.2 fusion.64
  34.7 5.0 convert_reduce_fusion.3
  40.0 5.2 fusion.64
  45.2 5.0 convert_reduce_fusion.3
  50.4 5.2 fusion.64
  55.6 5.0 convert_reduce_fusion.3
  60.9 5.2 fusion.64
  66.1 5.0 convert_reduce_fusion.3
  71.4 5.2 fusion.64
  76.6 5.0 convert_reduce_fusion.3
  81.8 5.2 fusion.64
  87.0 5.0 convert_reduce_fusion.3
  92.3 5.2 fusion.64
  97.5 5.0 convert_reduce_fusion.3
  102.7 5.2 fusion.64
  113.2 5.2 fusion.64
  118.4 5.0 convert_reduce_fusion.3
  123.7 5.3 fusion.64
  134.2 5.2 fusion.64
  139.4 5.0 convert_reduce_fusion.3
  144.7 5.2 fusion.64
  155.2 5.2 fusion.64
  165.6 5.2 fusion.64
  176.0 5.2 fusion.64
  186.5 5.3 fusion.64
  197.0 5.2 fusion.64
  202.3 5.0 convert_reduce_fusion.3
  207.5 5.2 fusion.64
  212.7 5.0 convert_reduce_fusion.3
  218.0 5.2 fusion.64
  228.5 5.2 fusion.64
  239.0 5.2 fusion.64
  244.2 5.0 convert_reduce_fusion.3
  249.4 5.3 fusion.64
  259.9 5.2 fusion.64
  265.1 5.0 convert_reduce_fusion.3
  270.4 5.2 fusion.64
  280.9 5.2 fusion.64
  291.3 5.2 fusion.64
  296.5 5.0 convert_reduce_fusion.3
  301.7 5.2 fusion.64
  306.9 5.0 convert_reduce_fusion.3
  314.5 13.0 %convolution_bitcast_fusion.4 = f32[4,32,128]{2,0,1:T(4,128)S(1)} fusion(bf16[27,32,128,128]{3,2,0,1:T(8,128)(2,1)} %get-tuple-element.243, bf16[27,8,32,128]{3,1,0,2:T(8,128)(2,1)S(1)} %constant_dynamic-update-slice_fusion), kind=kOutput, calls=%fused_computation.37 | convolution fusion | flops 113246208 | bytes 29261824 | tf_op jit(solution)/shard_map/otij,oftj->fti/dot_general | solution.py:155
  327.5 13.2 %convolution_bitcast_fusion.5 = f32[4,32,128]{2,0,1:T(4,128)S(1)} fusion(bf16[27,32,128,128]{3,2,0,1:T(8,128)(2,1)} %get-tuple-element.241, bf16[27,8,32,128]{3,1,0,2:T(8,128)(2,1)S(1)} %constant_dynamic-update-slice_fusion), kind=kOutput, calls=%fused_computation.38 | convolution fusion | flops 113246208 | bytes 29261824 | tf_op jit(solution)/shard_map/otij,oftj->fti/dot_general | solution.py:152
  341.3 16.6 %all-reduce.2 = (f32[2]{0:T(128)S(1)}, f32[2]{0:T(128)S(1)}) all-reduce(f32[2]{0:T(128)S(1)} %reduce_sum.132, f32[2]{0:T(128)S(1)} %reduce_sum.135), channel_id=1, replica_groups=mesh['gx'=8,'gy_0'=4,'gy_1'=2,'gz'=4] {'gx'}, use_global_device_ids=true, to_apply=%region_2.3 | all-reduce | flops 4 | bytes 32 | tf_op jit(solution)/shard_map/psum | solution.py:32
  357.9 7.4 %all-reduce.8 = (f32[2]{0:T(128)S(1)}, f32[2]{0:T(128)S(1)}) all-reduce(f32[2]{0:T(128)S(1)} %get-tuple-element.295, f32[2]{0:T(128)S(1)} %get-tuple-element.296), channel_id=1, replica_groups=mesh['gx'=8,'gy_0'=4,'gy_1'=2,'gz'=4] {'gy_0'}, use_global_device_ids=true, to_apply=%region_3.4 | all-reduce | flops 4 | bytes 32 | tf_op jit(solution)/shard_map/psum | solution.py:32
  365.3 11.5 %all-reduce.11 = (f32[2]{0:T(128)S(1)}, f32[2]{0:T(128)S(1)}) all-reduce(f32[2]{0:T(128)S(1)} %get-tuple-element.307, f32[2]{0:T(128)S(1)} %get-tuple-element.308), channel_id=1, replica_groups=mesh['gx'=8,'gy_0'=4,'gy_1'=2,'gz'=4] {'gy_1'}, use_global_device_ids=true, to_apply=%region_4.5 | all-reduce | flops 4 | bytes 32 | tf_op jit(solution)/shard_map/psum | solution.py:32
  376.8 9.6 %all-reduce.5 = (f32[2]{0:T(128)S(1)}, f32[2]{0:T(128)S(1)}) all-reduce(f32[2]{0:T(128)S(1)} %get-tuple-element.313, f32[2]{0:T(128)S(1)} %get-tuple-element.314), channel_id=1, replica_groups=mesh['gx'=8,'gy_0'=4,'gy_1'=2,'gz'=4] {'gz'}, use_global_device_ids=true, to_apply=%region_5.6 | all-reduce | flops 4 | bytes 32 | tf_op jit(solution)/shard_map/psum | solution.py:32
  393.0 5.4 collective-permute-start.9
  410.5 13.0 %convolution_bitcast_fusion.2 = f32[4,32,128]{2,0,1:T(4,128)S(1)} fusion(bf16[27,32,128,128]{3,2,0,1:T(8,128)(2,1)} %get-tuple-element.243, bf16[27,8,32,128]{3,1,0,2:T(8,128)(2,1)S(1)} %constant_dynamic-update-slice_fusion.29), kind=kOutput, calls=%fused_computation.35 | convolution fusion | flops 113246208 | bytes 29261824 | tf_op jit(solution)/shard_map/otij,oftj->fti/dot_general | solution.py:155
  423.6 13.2 %convolution_bitcast_fusion.3 = f32[4,32,128]{2,0,1:T(4,128)S(1)} fusion(bf16[27,32,128,128]{3,2,0,1:T(8,128)(2,1)} %get-tuple-element.241, bf16[27,8,32,128]{3,1,0,2:T(8,128)(2,1)S(1)} %constant_dynamic-update-slice_fusion.29), kind=kOutput, calls=%fused_computation.36 | convolution fusion | flops 113246208 | bytes 29261824 | tf_op jit(solution)/shard_map/otij,oftj->fti/dot_general | solution.py:152
  437.1 12.9 %all-reduce.1 = (f32[2]{0:T(128)S(1)}, f32[2]{0:T(128)S(1)}) all-reduce(f32[2]{0:T(128)S(1)} %reduce_sum.138, f32[2]{0:T(128)S(1)} %reduce_sum.141), channel_id=1, replica_groups=mesh['gx'=8,'gy_0'=4,'gy_1'=2,'gz'=4] {'gx'}, use_global_device_ids=true, to_apply=%region_18.19 | all-reduce | flops 4 | bytes 32 | tf_op jit(solution)/shard_map/psum | solution.py:32
  450.0 6.0 %all-reduce.7 = (f32[2]{0:T(128)S(1)}, f32[2]{0:T(128)S(1)}) all-reduce(f32[2]{0:T(128)S(1)} %get-tuple-element.293, f32[2]{0:T(128)S(1)} %get-tuple-element.294), channel_id=1, replica_groups=mesh['gx'=8,'gy_0'=4,'gy_1'=2,'gz'=4] {'gy_0'}, use_global_device_ids=true, to_apply=%region_19.20 | all-reduce | flops 4 | bytes 32 | tf_op jit(solution)/shard_map/psum | solution.py:32
  456.0 11.3 %all-reduce.10 = (f32[2]{0:T(128)S(1)}, f32[2]{0:T(128)S(1)}) all-reduce(f32[2]{0:T(128)S(1)} %get-tuple-element.305, f32[2]{0:T(128)S(1)} %get-tuple-element.306), channel_id=1, replica_groups=mesh['gx'=8,'gy_0'=4,'gy_1'=2,'gz'=4] {'gy_1'}, use_global_device_ids=true, to_apply=%region_20.21 | all-reduce | flops 4 | bytes 32 | tf_op jit(solution)/shard_map/psum | solution.py:32
  467.3 8.0 %all-reduce.4 = (f32[2]{0:T(128)S(1)}, f32[2]{0:T(128)S(1)}) all-reduce(f32[2]{0:T(128)S(1)} %get-tuple-element.311, f32[2]{0:T(128)S(1)} %get-tuple-element.312), channel_id=1, replica_groups=mesh['gx'=8,'gy_0'=4,'gy_1'=2,'gz'=4] {'gz'}, use_global_device_ids=true, to_apply=%region_21.22 | all-reduce | flops 4 | bytes 32 | tf_op jit(solution)/shard_map/psum | solution.py:32
  482.1 5.4 collective-permute-start.15
  499.6 13.0 %convolution_bitcast_fusion = f32[4,32,128]{2,0,1:T(4,128)S(1)} fusion(bf16[27,32,128,128]{3,2,0,1:T(8,128)(2,1)} %get-tuple-element.243, bf16[27,8,32,128]{3,1,0,2:T(8,128)(2,1)S(1)} %constant_dynamic-update-slice_fusion.58), kind=kOutput, calls=%fused_computation.33 | convolution fusion | flops 113246208 | bytes 29261824 | tf_op jit(solution)/shard_map/otij,oftj->fti/dot_general | solution.py:155
  512.6 13.2 %convolution_bitcast_fusion.1 = f32[4,32,128]{2,0,1:T(4,128)S(1)} fusion(bf16[27,32,128,128]{3,2,0,1:T(8,128)(2,1)} %get-tuple-element.241, bf16[27,8,32,128]{3,1,0,2:T(8,128)(2,1)S(1)} %constant_dynamic-update-slice_fusion.58), kind=kOutput, calls=%fused_computation.34 | convolution fusion | flops 113246208 | bytes 29261824 | tf_op jit(solution)/shard_map/otij,oftj->fti/dot_general | solution.py:152
  526.2 13.2 %all-reduce = (f32[2]{0:T(128)S(1)}, f32[2]{0:T(128)S(1)}) all-reduce(f32[2]{0:T(128)S(1)} %reduce_sum.144, f32[2]{0:T(128)S(1)} %reduce_sum.147), channel_id=1, replica_groups=mesh['gx'=8,'gy_0'=4,'gy_1'=2,'gz'=4] {'gx'}, use_global_device_ids=true, to_apply=%region_30.31 | all-reduce | flops 4 | bytes 32 | tf_op jit(solution)/shard_map/psum | solution.py:32
  539.4 6.1 %all-reduce.6 = (f32[2]{0:T(128)S(1)}, f32[2]{0:T(128)S(1)}) all-reduce(f32[2]{0:T(128)S(1)} %get-tuple-element.291, f32[2]{0:T(128)S(1)} %get-tuple-element.292), channel_id=1, replica_groups=mesh['gx'=8,'gy_0'=4,'gy_1'=2,'gz'=4] {'gy_0'}, use_global_device_ids=true, to_apply=%region_31.32 | all-reduce | flops 4 | bytes 32 | tf_op jit(solution)/shard_map/psum | solution.py:32
  545.5 11.4 %all-reduce.9 = (f32[2]{0:T(128)S(1)}, f32[2]{0:T(128)S(1)}) all-reduce(f32[2]{0:T(128)S(1)} %get-tuple-element.303, f32[2]{0:T(128)S(1)} %get-tuple-element.304), channel_id=1, replica_groups=mesh['gx'=8,'gy_0'=4,'gy_1'=2,'gz'=4] {'gy_1'}, use_global_device_ids=true, to_apply=%region_32.33 | all-reduce | flops 4 | bytes 32 | tf_op jit(solution)/shard_map/psum | solution.py:32
  556.8 8.0 %all-reduce.3 = (f32[2]{0:T(128)S(1)}, f32[2]{0:T(128)S(1)}) all-reduce(f32[2]{0:T(128)S(1)} %get-tuple-element.309, f32[2]{0:T(128)S(1)} %get-tuple-element.310), channel_id=1, replica_groups=mesh['gx'=8,'gy_0'=4,'gy_1'=2,'gz'=4] {'gz'}, use_global_device_ids=true, to_apply=%region_33.34 | all-reduce | flops 4 | bytes 32 | tf_op jit(solution)/shard_map/psum | solution.py:32
  (445 shorter events, 126.2 us)
Async XLA Ops:
  0.6 16.8 %copy-start = (f32[4,2,2,8,128]{4,3,2,1,0:T(8,128)S(1)}, f32[4,2,2,8,128]{4,3,2,1,0:T(8,128)}, u32[]{:S(2)}) copy-start(f32[4,2,2,8,128]{4,3,2,1,0:T(8,128)} %param.17) | copy-start | bytes 196612
  0.6 18.8 %copy-start.3 = (f32[2,2,8,128]{3,2,1,0:T(8,128)S(1)}, f32[2,2,8,128]{3,2,1,0:T(8,128)}, u32[]{:S(2)}) copy-start(f32[2,2,8,128]{3,2,1,0:T(8,128)} %param.12) | copy-start | bytes 49156
  0.7 18.8 %copy-start.4 = (f32[2,2,8,128]{3,2,1,0:T(8,128)S(1)}, f32[2,2,8,128]{3,2,1,0:T(8,128)}, u32[]{:S(2)}) copy-start(f32[2,2,8,128]{3,2,1,0:T(8,128)} %param.11) | copy-start | bytes 49156
  0.7 18.8 %copy-start.2 = (f32[3,2,2,8,128]{4,3,2,1,0:T(8,128)S(1)}, f32[3,2,2,8,128]{4,3,2,1,0:T(8,128)}, u32[]{:S(2)}) copy-start(f32[3,2,2,8,128]{4,3,2,1,0:T(8,128)} %param.10) | copy-start | bytes 147460
  1.6 7.1 %collective-permute-start.1 = (f32[9,1,2,8,128]{4,3,2,1,0:T(8,128)S(1)}, f32[9,1,2,8,128]{4,3,2,1,0:T(8,128)S(1)}, u32[]{:S(2)}, u32[]{:S(2)}) collective-permute-start(f32[9,1,2,8,128]{4,3,2,1,0:T(8,128)S(1)} %get-tuple-element.438), channel_id=1, source_target_pairs={{32,0},{64,32},{96,64},{128,96},{160,128},{192,160},{224,192},{33,... | collective-permute-start | bytes 221192 | tf_op jit(solution)/shard_map/ppermute | solution.py:26
  2.9 6.4 %collective-permute-start = (f32[9,1,2,8,128]{4,3,2,1,0:T(8,128)S(1)}, f32[9,1,2,8,128]{4,3,2,1,0:T(8,128)S(1)}, u32[]{:S(2)}, u32[]{:S(2)}) collective-permute-start(f32[9,1,2,8,128]{4,3,2,1,0:T(8,128)S(1)} %get-tuple-element.437), channel_id=1, source_target_pairs={{0,32},{32,64},{64,96},{96,128},{128,160},{160,192},{192,224},{1,3... | collective-permute-start | bytes 221192 | tf_op jit(solution)/shard_map/ppermute | solution.py:23
  10.2 7.9 %collective-permute-start.3 = (f32[9,4,1,8,128]{4,3,2,1,0:T(8,128)S(1)}, f32[9,4,1,8,128]{4,3,2,1,0:T(8,128)S(1)}, u32[]{:S(2)}, u32[]{:S(2)}) collective-permute-start(f32[9,4,1,8,128]{4,3,2,1,0:T(8,128)S(1)} %get-tuple-element.420), channel_id=1, source_target_pairs={{4,0},{8,4},{12,8},{16,12},{20,16},{24,20},{28,24},{5,1},{9,5},{13... | collective-permute-start | bytes 442376 | tf_op jit(solution)/shard_map/ppermute | solution.py:26
  15.5 4.0 collective-permute-start.2
  19.6 5.9 %collective-permute-start.5 = (f32[9,4,4,1,128]{4,3,2,1,0:T(1,128)S(1)}, f32[9,4,4,1,128]{4,3,2,1,0:T(1,128)S(1)}, u32[]{:S(2)}, u32[]{:S(2)}) collective-permute-start(f32[9,4,4,1,128]{4,3,2,1,0:T(1,128)S(1)} %get-tuple-element.337), channel_id=1, source_target_pairs={{1,0},{2,1},{3,2},{5,4},{6,5},{7,6},{9,8},{10,9},{11,10},{13,12},{... | collective-permute-start | bytes 221192 | tf_op jit(solution)/shard_map/ppermute | solution.py:26
  20.9 5.9 %collective-permute-start.4 = (f32[9,4,4,1,128]{4,3,2,1,0:T(1,128)S(1)}, f32[9,4,4,1,128]{4,3,2,1,0:T(1,128)S(1)}, u32[]{:S(2)}, u32[]{:S(2)}) collective-permute-start(f32[9,4,4,1,128]{4,3,2,1,0:T(1,128)S(1)} %get-tuple-element.336), channel_id=1, source_target_pairs={{0,1},{1,2},{2,3},{4,5},{5,6},{6,7},{8,9},{9,10},{10,11},{12,13},{... | collective-permute-start | bytes 221192 | tf_op jit(solution)/shard_map/ppermute | solution.py:23
  27.1 1.0 copy-start.1
  28.3 1.1 slice-start
  327.5 13.2 %copy-start.7 = (f32[2,2,8,128]{3,2,1,0:T(8,128)S(1)}, f32[2,2,8,128]{3,2,1,0:T(8,128)}, u32[]{:S(2)}) copy-start(f32[2,2,8,128]{3,2,1,0:T(8,128)} %param.14) | copy-start | bytes 49156
  327.5 13.2 %copy-start.8 = (f32[2,2,8,128]{3,2,1,0:T(8,128)S(1)}, f32[2,2,8,128]{3,2,1,0:T(8,128)}, u32[]{:S(2)}) copy-start(f32[2,2,8,128]{3,2,1,0:T(8,128)} %param.13) | copy-start | bytes 49156
  327.5 13.3 %copy-start.5 = (f32[2,2,8,128]{3,2,1,0:T(8,128)S(1)}, f32[2,2,8,128]{3,2,1,0:T(8,128)}, u32[]{:S(2)}) copy-start(f32[2,2,8,128]{3,2,1,0:T(8,128)} %param.15) | copy-start | bytes 49156
  327.5 13.3 %copy-start.6 = (f32[2,2,2,8,128]{4,0,3,2,1:T(2,128)S(1)}, f32[2,2,2,8,128]{4,0,3,2,1:T(2,128)}, u32[]{:S(2)}) copy-start(f32[2,2,2,8,128]{4,0,3,2,1:T(2,128)} %copy.110) | copy-start | bytes 98308
  386.7 5.3 collective-permute-start.7
  388.0 5.0 collective-permute-start.6
  393.0 7.4 %collective-permute-start.9 = (f32[4,4,1,8,128]{4,3,2,1,0:T(8,128)S(1)}, f32[4,4,1,8,128]{4,3,2,1,0:T(8,128)S(1)}, u32[]{:S(2)}, u32[]{:S(2)}) collective-permute-start(f32[4,4,1,8,128]{4,3,2,1,0:T(8,128)S(1)} %get-tuple-element.442), channel_id=1, source_target_pairs={{4,0},{8,4},{12,8},{16,12},{20,16},{24,20},{28,24},{5,1},{9,5},{13... | collective-permute-start | bytes 196616 | tf_op jit(solution)/shard_map/ppermute | solution.py:26
  398.5 3.2 collective-permute-start.8
  401.7 5.7 %collective-permute-start.11 = (f32[4,4,4,1,128]{4,3,2,1,0:T(1,128)S(1)}, f32[4,4,4,1,128]{4,3,2,1,0:T(1,128)S(1)}, u32[]{:S(2)}, u32[]{:S(2)}) collective-permute-start(f32[4,4,4,1,128]{4,3,2,1,0:T(1,128)S(1)} %get-tuple-element.432), channel_id=1, source_target_pairs={{1,0},{2,1},{3,2},{5,4},{6,5},{7,6},{9,8},{10,9},{11,10},{13,12},{... | collective-permute-start | bytes 98312 | tf_op jit(solution)/shard_map/ppermute | solution.py:26
  403.0 5.0 collective-permute-start.10
  475.8 5.3 collective-permute-start.13
  477.1 5.0 collective-permute-start.12
  482.1 7.3 %collective-permute-start.15 = (f32[4,4,1,8,128]{4,3,2,1,0:T(8,128)S(1)}, f32[4,4,1,8,128]{4,3,2,1,0:T(8,128)S(1)}, u32[]{:S(2)}, u32[]{:S(2)}) collective-permute-start(f32[4,4,1,8,128]{4,3,2,1,0:T(8,128)S(1)} %get-tuple-element.440), channel_id=1, source_target_pairs={{4,0},{8,4},{12,8},{16,12},{20,16},{24,20},{28,24},{5,1},{9,5},{13... | collective-permute-start | bytes 196616 | tf_op jit(solution)/shard_map/ppermute | solution.py:26
  487.5 3.2 collective-permute-start.14
  490.8 5.4 collective-permute-start.17
  492.1 5.0 collective-permute-start.16
where the time goes:
time: 567 us; the launch traced here: 566 us
  other arithmetic  283 us (50%)
  blocking collectives  122 us (22%)
  matrix products  78.7 us (14%)
  starting transfers between devices  54.7 us (10%)
  local copies, waits for them, and re-layouts  11 us (2%)
  waiting for transfers between devices  9.94 us (2%)
    dynamic_update_slice x27, other arithmetic, build(): lax.dynamic_update_index_in_dim(store_response, response, offset_code, 0)  141 us
    reduce_sum x27, other arithmetic, build(): row_response = row_response + jnp.sum(response.astype(jnp.float32), axis=2)  135 us
    psum x12, blocking collectives, one_axis_at_a_time(): return functools.reduce(lax.psum, axes, shard)  122 us
    dot_general x3, matrix products, operate(): jnp.einsum('otij,oftj->fti', store_coulomb, stacked[:, :4], preferred_ele...  39.6 us
    dot_general x3, matrix products, operate(): jnp.einsum('otij,oftj->fti', store_response, stacked[:, 4:], preferred_el...  39.1 us
    ppermute x9, starting transfers between devices, extended(): lax.ppermute(lax.slice_in_dim(block, block.shape[dim] - width, None, axis...  30.9 us
    ppermute x9, starting transfers between devices, extended(): lax.ppermute(lax.slice_in_dim(block, 0, width, axis=dim), axis, backward)  23.8 us
  transfers between devices with their start and end apart: 18, of which 10 were waited for; matrix products, arithmetic and copies ran while one was open for 0% of the time, Pallas kernels for 0%

commit v1 on v0

v1 whole, which is shorter than its diff:
```python
import itertools

import jax
import jax.numpy as jnp
from jax import lax
from jax.experimental import pallas as pl
from jax.experimental.pallas import tpu as pltpu
from jax.sharding import PartitionSpec as P

MESH = pl.DeviceIdType.MESH
AXES = ("gx", "gy", "gz")
BF = jnp.bfloat16
F32 = jnp.float32
SHIFT = 4.0
LOG2E = 1.4426950408889634
COULOMB_GAIN = 250000.0
RESPONSE_SCALE = 0.003
GROUP = 8
WIDE = 16
DIRECTIONS = [d for d in itertools.product((-1, 0, 1), repeat=3) if d != (0, 0, 0)]
VMEM_SPEC = pl.BlockSpec(memory_space=pltpu.VMEM)
SMEM_SPEC = pl.BlockSpec(memory_space=pltpu.SMEM)


def own_range(step, size):
    return pl.ds(0, size) if step == 0 else pl.ds(size - 1 if step > 0 else 0, 1)


def ghost_range(step, size):
    return pl.ds(1, size) if step == 0 else pl.ds(0 if step > 0 else size + 1, 1)


def neighbour(direction):
    exists = None
    place = []
    for axis, step in zip(AXES, direction):
        at = lax.axis_index(axis) + step
        place.append(at)
        if step:
            inside = at >= 0 if step < 0 else at < lax.axis_size(axis)
            exists = inside if exists is None else exists & inside
    return tuple(place), exists


def greet():
    barrier = pltpu.get_barrier_semaphore()
    count = jnp.int32(0)
    for direction in DIRECTIONS:
        place, exists = neighbour(direction)

        @pl.when(exists)
        def _():
            pl.semaphore_signal(barrier, inc=1, device_id=place, device_id_type=MESH)

        count = count + exists.astype(jnp.int32)
    return barrier, count


def exchange(pairs, send_sem, recv_sem):
    def copies(index, direction, place):
        made = []
        for number, (own, ext) in enumerate(pairs):
            size = own.shape[:3]
            source = own.at[tuple(own_range(s, n) for s, n in zip(direction, size))]
            target = ext.at[tuple(ghost_range(s, n) for s, n in zip(direction, size))]
            made.append(
                pltpu.make_async_remote_copy(
                    source,
                    target,
                    send_sem.at[number, index],
                    recv_sem.at[number, index],
                    device_id=place,
                    device_id_type=MESH,
                )
            )
        return made

    for index, direction in enumerate(DIRECTIONS):
        place, exists = neighbour(direction)

        @pl.when(exists)
        def _():
            for copy in copies(index, direction, place):
                copy.start()

    for index, direction in enumerate(DIRECTIONS):
        place, exists = neighbour(direction)
        source, incoming = neighbour(tuple(-s for s in direction))

        @pl.when(incoming)
        def _():
            for copy in copies(index, direction, place):
                copy.wait_recv()

        @pl.when(exists)
        def _():
            for copy in copies(index, direction, place):
                copy.wait_send()


def first_halo(pos, shield, width, rhs, param_ext, field_ext, param_own, field_own, send_sem, recv_sem):
    param_ext[...] = jnp.zeros_like(param_ext)
    field_ext[...] = jnp.zeros_like(field_ext)
    barrier, count = greet()
    nx, ny, nz = shield.shape[:3]
    for x in range(nx):
        for y in range(ny):
            columns = [pos[0, x, y], pos[1, x, y], pos[2, x, y], shield[x, y], width[x, y]]
            fields = [rhs[f, x, y] for f in range(4)]
            for z in range(nz):
                for f in range(5):
                    row = columns[f][z : z + 1]
                    param_own[x, y, z, f : f + 1, :] = row
                    param_ext[x + 1, y + 1, z + 1, f : f + 1, :] = row
                param_own[x, y, z, 5:8, :] = jnp.zeros((3, 128), F32)
                for f in range(4):
                    row = fields[f][z : z + 1]
                    field_own[x, y, z, f : f + 1, :] = row
                    field_ext[x + 1, y + 1, z + 1, f : f + 1, :] = row
    pl.semaphore_wait(barrier, count)
    exchange(((param_own, param_ext), (field_own, field_ext)), send_sem, recv_sem)


def next_halo(own, ext, send_sem, recv_sem):
    ext[...] = jnp.zeros_like(ext)
    barrier, count = greet()
    ext[1:-1, 1:-1, 1:-1] = own[...]
    pl.semaphore_wait(barrier, count)
    exchange(((own, ext),), send_sem, recv_sem)


def split3(value):
    first = value.astype(BF)
    rest = value - first.astype(F32)
    second = rest.astype(BF)
    third = (rest - second.astype(F32)).astype(BF)
    return first.astype(F32), second.astype(F32), third.astype(F32)


def rows_of(pieces):
    row = lax.broadcasted_iota(jnp.int32, (8, 128), 0)
    value = jnp.zeros((8, 128), F32)
    for index, piece in pieces:
        value = jnp.where(row == index, piece, value)
    return value


def centred(param, ex, ey, ez, half):
    row = lax.broadcasted_iota(jnp.int32, (8, 128), 0)
    offset = jnp.where(row == 0, ex, jnp.where(row == 1, ey, ez)).astype(F32) - jnp.where(
        row == 0, half[0], jnp.where(row == 1, half[1], half[2])
    )
    place = param + offset
    square = jnp.sum(jnp.where(row < 3, place * place, 0.0), axis=0, keepdims=True)
    return row, place, jnp.broadcast_to(square, (8, 128))


def partner_features(param, ex, ey, ez, half):
    row, place, square = centred(param, ex, ey, ez, half)
    value = jnp.where(row < 3, place, jnp.where(row == 3, param, 0.0))
    value = jnp.where(row == 4, square, jnp.where(row == 5, 1.0, value))
    one, two, three = split3(value)
    return jnp.concatenate([one, two, one, two, three, one], axis=0)


def own_features(param, ex, ey, ez, half):
    row, place, square = centred(param, ex, ey, ez, half)
    sides = []
    for gain, shielded in ((-LOG2E, 0.0), (COULOMB_GAIN, COULOMB_GAIN)):
        value = jnp.where(row < 3, (-2.0 * gain) * place, jnp.where(row == 3, shielded * param, 0.0))
        value = jnp.where(row == 4, gain, jnp.where(row == 5, gain * square, value))
        one, two, three = split3(value)
        sides.append(jnp.concatenate([one, one, two, two, one, three], axis=0))
    return jnp.concatenate(sides, axis=1)


def split_fields(ext, halves, tiles):
    ones = jnp.ones((8, 128), F32)

    def step(index, carry):
        for sub in range(8):
            e = index * 8 + sub
            value = ext[e]
            high = value.astype(BF).astype(F32)
            low = value - high
            halves[e] = jnp.concatenate([high, low, ones], axis=0).astype(BF)
        return carry

    lax.fori_loop(0, tiles // 8, step, 0)


def apply_pairs(groups, entries, halves, store, acc):
    acc[...] = jnp.zeros_like(acc)

    def step(index, carry):
        for sub in range(WIDE):
            slot = index * WIDE + sub
            code = entries[slot]
            e = code & 255
            t = lax.shift_right_logical(code, 16)
            both = jnp.concatenate([store[slot, 0], store[slot, 1]], axis=1)
            out = jnp.dot(halves[e], both, preferred_element_type=F32)
            acc[t] = acc[t] + out
        return carry

    lax.fori_loop(0, groups, step, 0)


def diagonal_image(t, out, diagonal, coupling, vector):
    row = lax.broadcasted_iota(jnp.int32, (4, 128), 0)
    summed = out[0:4] + out[4:8]
    pair = jnp.where(row < 2, summed[:, :128], -summed[:, 128:])
    value = vector[t]
    swapped = jnp.concatenate([value[2:4], value[0:2]], axis=0)
    return diagonal * value + pair + coupling[t // 8, pl.ds(t % 8, 1), :] * swapped


def build(
    bits, param, field, own, hardness, softness, coupling, blank, store, entries, count, diagonal, image, send,
    features, mine, halves, acc
):
    ex_size, ey_size, ez_size = 4, 4, 10
    half = (2.0, 2.0, 5.0)
    tiles = ex_size * ey_size * ez_size
    owned = 32

    def features_step(index, carry):
        for sub in range(4):
            e = index * 4 + sub
            ex = e // (ey_size * ez_size)
            ey = (e // ez_size) % ey_size
            ez = e % ez_size
            rows = partner_features(param[e], ex, ey, ez, half)
            features[e, :, 0:48] = rows.T.astype(BF)
        return carry

    lax.fori_loop(0, tiles // 4, features_step, 0)

    def own_step(index, carry):
        for sub in range(2):
            t = index * 2 + sub
            ex = t // 16 + 1
            ey = (t // 8) % 2 + 1
            ez = t % 8 + 1
            e = (ex * ey_size + ey) * ez_size + ez
            mine[t] = own_features(param[e], ex, ey, ez, half).astype(BF)
            entries[t] = e + 256 * t + 65536 * t
        return carry

    lax.fori_loop(0, owned // 2, own_step, 0)
    split_fields(field, halves, tiles)

    def list_step(t, at):
        ex = t // 16 + 1
        ey = (t // 8) % 2 + 1
        ez = t % 8 + 1
        e = (ex * ey_size + ey) * ez_size + ez
        word = bits[t]
        for code in range(27):
            if code == 13:
                continue
            shift = ((code // 9 - 1) * ey_size + (code // 3 % 3 - 1)) * ez_size + code % 3 - 1
            entries[at] = (e + shift) + 256 * t + 65536 * t
            at = at + (lax.shift_right_logical(word, code) & 1)
        return at

    total = lax.fori_loop(0, owned, list_step, jnp.int32(owned))
    middle = (ey_size + 1) * ez_size + 1
    for sub in range(WIDE):
        entries[total + sub] = middle + 65536 * owned
    count[0] = total

    def pair(slot, masked):
        code = entries[slot]
        e = code & 255
        t = lax.shift_right_logical(code, 8) & 255
        both = jnp.dot(features[e, :, 0:48], mine[t], preferred_element_type=F32)
        width_row = param[e, 4:5, :]
        partner_width = jnp.broadcast_to(width_row, (128, 128)).T
        ex = t // 16 + 1
        ey = (t // 8) % 2 + 1
        ez = t % 8 + 1
        here = (ex * ey_size + ey) * ez_size + ez
        widths = partner_width + param[here, 4:5, :]
        coulomb = lax.rsqrt(both[:, 128:])
        response = RESPONSE_SCALE * jnp.exp2(both[:, :128] / widths)
        if masked:
            same = lax.broadcasted_iota(jnp.int32, (128, 128), 0) == lax.broadcasted_iota(
                jnp.int32, (128, 128), 1
            )
            coulomb = jnp.where(same, 0.0, coulomb)
            response = jnp.where(same, 0.0, response)
        store[slot, 0] = coulomb.astype(BF)
        store[slot, 1] = response.astype(BF)

    def self_step(index, carry):
        for sub in range(4):
            pair(index * 4 + sub, True)
        return carry

    lax.fori_loop(0, owned // 4, self_step, 0)

    def pair_step(index, carry):
        for sub in range(GROUP):
            pair(owned + index * GROUP + sub, False)
        return carry

    lax.fori_loop(0, (total - owned + GROUP - 1) // GROUP, pair_step, 0)
    apply_pairs((total + WIDE - 1) // WIDE, entries, halves, store, acc)

    row = lax.broadcasted_iota(jnp.int32, (4, 128), 0)

    def finish(t, carry):
        out = acc[t]
        a, b = t // 8, pl.ds(t % 8, 1)
        top = hardness[a, b, :] + out[8:9, :128]
        low = softness[a, b, :] + out[8:9, 128:]
        diag = jnp.where(row < 2, top, low)
        diagonal[t] = diag
        value = diagonal_image(t, out, diag, coupling, own)
        image[t] = value
        send[t] = value - SHIFT * own[t]
        return carry

    lax.fori_loop(0, owned, finish, 0)


def again(field, own, coupling, store, entries, count, diagonal, image, send, passed, halves, acc):
    owned = 32
    split_fields(field, halves, field.shape[0])
    apply_pairs((count[0] + WIDE - 1) // WIDE, entries, halves, store, acc)

    def finish(t, carry):
        value = diagonal_image(t, acc[t], diagonal[t], coupling, own)
        image[t] = value
        send[t] = value - SHIFT * own[t]
        return carry

    lax.fori_loop(0, owned, finish, 0)


def combine(u0, u1, u2, w0, w1, w2, solution, residual, part, stage, send_sem, recv_sem):
    basis = (u0, u1, u2)
    images = (w0, w1, w2)
    sizes = [lax.axis_size(axis) for axis in AXES]
    places = [lax.axis_index(axis) for axis in AXES]
    barrier = pltpu.get_barrier_semaphore()
    for which, size in enumerate(sizes):
        for step in range(1, size):
            peer = list(places)
            peer[which] = lax.rem(places[which] + step, size)
            pl.semaphore_signal(barrier, inc=1, device_id=tuple(peer), device_id_type=MESH)

    wanted = [(u0, u0), (u0, u1), (u0, u2), (u0, w0), (u0, w1), (u0, w2), (u1, w1), (u1, w2), (u2, w2)]
    sums = []
    for left, right in wanted:
        both = jnp.sum(left[...] * right[...], axis=0)
        sums.append(both[0:2] + both[2:4])
    lane = lax.broadcasted_iota(jnp.int32, (8, 128), 1)
    packed = jnp.zeros((8, 128), F32)
    for block in range(3):
        rows = sums[4 * block : 4 * block + 4]
        rows = rows + [jnp.zeros((2, 128), F32)] * (4 - len(rows))
        folded = jnp.concatenate(rows, axis=0)
        folded = folded + pltpu.roll(folded, 64, 1)
        folded = folded + pltpu.roll(folded, 32, 1)
        packed = jnp.where((lane >= 32 * block) & (lane < 32 * block + 32), folded, packed)
    part[0] = packed
    pl.semaphore_wait(barrier, sum(size - 1 for size in sizes))

    for turn, which in enumerate((2, 1, 0)):
        size = sizes[which]
        made = []
        for step in range(1, size):
            peer = list(places)
            peer[which] = lax.rem(places[which] + step, size)
            copy = pltpu.make_async_remote_copy(
                part.at[turn],
                stage.at[turn, step - 1],
                send_sem.at[turn, step - 1],
                recv_sem.at[turn, step - 1],
                device_id=tuple(peer),
                device_id_type=MESH,
            )
            copy.start()
            made.append(copy)
        mine = part[turn]
        for copy in made:
            copy.wait_recv()
        received = [mine] + [stage[turn, step - 1] for step in range(1, size)]
        total = jnp.zeros((8, 128), F32)
        for place in range(size):
            term = jnp.zeros((8, 128), F32)
            for step in range(size):
                term = jnp.where(lax.rem(places[which] - step + size, size) == place, received[step], term)
            total = total + term
        for copy in made:
            copy.wait_send()
        part[turn + 1] = total

    total = part[3]
    gram = {}
    values = []
    for block in range(3):
        inside = (lane >= 32 * block) & (lane < 32 * block + 32)
        values.append(jnp.sum(jnp.where(inside, total, 0.0), axis=1, keepdims=True))
    value = []
    for index in range(9):
        two = values[index // 4][2 * (index % 4) : 2 * (index % 4) + 2]
        value.append(jnp.concatenate([two, two], axis=0))
    m0, m1, m2, g00, g01, g02, g11, g12, g22 = value
    f1 = g01 / g00
    f2 = g02 / g00
    h11 = g11 - f1 * g01
    h12 = g12 - f1 * g02
    h22 = g22 - f2 * g02
    n1 = m1 - f1 * m0
    n2 = m2 - f2 * m0
    f3 = h12 / h11
    k22 = h22 - f3 * h12
    k2 = n2 - f3 * n1
    c2 = k2 / k22
    c1 = (n1 - h12 * c2) / h11
    c0 = (m0 - g01 * c1 - g02 * c2) / g00
    c0, c1, c2 = (jnp.broadcast_to(c, (4, 128))[None] for c in (c0, c1, c2))
    answer = c0 * u0[...] + c1 * u1[...] + c2 * u2[...]
    left = u0[...] - (c0 * w0[...] + c1 * w1[...] + c2 * w2[...])
    for t in range(32):
        for f in range(4):
            solution[f, t // 8, t % 8 : t % 8 + 1, :] = answer[t, f : f + 1]
            residual[f, t // 8, t % 8 : t % 8 + 1, :] = left[t, f : f + 1]


def on_device(positions, shield, width, hardness, softness, coupling, pair_bits, right_side):
    nx, ny, nz, lanes = hardness.shape
    owned = nx * ny * nz
    ext = (nx + 2, ny + 2, nz + 2)
    tiles = ext[0] * ext[1] * ext[2]
    slots = owned * 27

    def kept(value):
        return pltpu.with_memory_space_constraint(value, pltpu.VMEM)

    def limits(size, **more):
        return pltpu.CompilerParams(vmem_limit_bytes=size, **more)

    param_ext, field_ext, field_own = pl.pallas_call(
        lambda pos, sh, wi, rhs, pe, fe, fo, po, ss, rs: first_halo(pos, sh, wi, rhs, pe, fe, po, fo, ss, rs),
        out_shape=(
            pltpu.VMEM(ext + (8, lanes), F32),
            pltpu.VMEM(ext + (4, lanes), F32),
            pltpu.VMEM((nx, ny, nz, 4, lanes), F32),
        ),
        in_specs=[VMEM_SPEC] * 4,
        out_specs=(VMEM_SPEC,) * 3,
        scratch_shapes=[
            pltpu.VMEM((nx, ny, nz, 8, lanes), F32),
            pltpu.SemaphoreType.DMA((2, 26)),
            pltpu.SemaphoreType.DMA((2, 26)),
        ],
        compiler_params=limits(4 << 20, collective_id=0, has_side_effects=True),
        name="first_halo",
    )(positions, shield, width, right_side)

    hard, soft, link = (a.reshape(owned // 8, 8, lanes) for a in (hardness, softness, coupling))
    own0 = field_own.reshape(owned, 4, lanes)
    vector = jax.ShapeDtypeStruct((owned, 4, lanes), F32)
    blank = pl.pallas_call(
        lambda ref: None,
        out_shape=pltpu.VMEM((slots, 2, lanes, lanes), BF),
        out_specs=VMEM_SPEC,
        compiler_params=limits(1 << 20),
        name="reserve",
    )()
    store, entries, count, diagonal, image0, own1 = pl.pallas_call(
        build,
        out_shape=(
            pltpu.VMEM((slots, 2, lanes, lanes), BF),
            jax.ShapeDtypeStruct((slots + 32,), jnp.int32),
            jax.ShapeDtypeStruct((1,), jnp.int32),
            jax.ShapeDtypeStruct((owned, 4, lanes), F32),
            jax.ShapeDtypeStruct((owned, 4, lanes), F32),
            jax.ShapeDtypeStruct((owned, 4, lanes), F32),
        ),
        in_specs=[SMEM_SPEC] + [VMEM_SPEC] * 7,
        input_output_aliases={7: 0},
        out_specs=(VMEM_SPEC, SMEM_SPEC, SMEM_SPEC, VMEM_SPEC, VMEM_SPEC, VMEM_SPEC),
        scratch_shapes=[
            pltpu.VMEM((tiles, lanes, lanes), BF),
            pltpu.VMEM((owned, 48, 2 * lanes), BF),
            pltpu.VMEM((tiles, 16, lanes), BF),
            pltpu.VMEM((owned + 1, 16, 2 * lanes), F32),
        ],
        compiler_params=limits(8 << 20),
        name="build",
    )(
        pair_bits.reshape(owned),
        kept(param_ext.reshape(tiles, 8, lanes)),
        kept(field_ext.reshape(tiles, 4, lanes)),
        own0,
        hard,
        soft,
        link,
        kept(blank),
    )

    def halo(own, number):
        return pl.pallas_call(
            next_halo,
            out_shape=jax.ShapeDtypeStruct(ext + (4, lanes), F32),
            in_specs=[VMEM_SPEC],
            out_specs=VMEM_SPEC,
            scratch_shapes=[pltpu.SemaphoreType.DMA((1, 26)), pltpu.SemaphoreType.DMA((1, 26))],
            compiler_params=limits(2 << 20, collective_id=number, has_side_effects=True),
            name="halo",
        )(own.reshape(nx, ny, nz, 4, lanes))

    def operate(own, store, number):
        field = halo(own, number)
        return pl.pallas_call(
            again,
            out_shape=(
                jax.ShapeDtypeStruct((owned, 4, lanes), F32),
                jax.ShapeDtypeStruct((owned, 4, lanes), F32),
                pltpu.VMEM(store.shape, BF),
            ),
            in_specs=[VMEM_SPEC] * 4 + [SMEM_SPEC] * 2 + [VMEM_SPEC],
            out_specs=(VMEM_SPEC,) * 3,
            input_output_aliases={3: 2},
            scratch_shapes=[
                pltpu.VMEM((tiles, 16, lanes), BF),
                pltpu.VMEM((owned + 1, 16, 2 * lanes), F32),
            ],
            compiler_params=limits(4 << 20),
            name="apply",
        )(field.reshape(tiles, 4, lanes), own, link, kept(store), entries, count, diagonal)

    image1, own2, store = operate(own1, store, 1)
    image2, _, _ = operate(own2, store, 2)
    sizes = [lax.axis_size(axis) for axis in AXES]
    most = max(sizes) - 1
    shape = jax.ShapeDtypeStruct((4, owned // 8, 8, lanes), F32)
    answer, left = pl.pallas_call(
        combine,
        out_shape=(shape, shape),
        in_specs=[VMEM_SPEC] * 6,
        out_specs=(VMEM_SPEC, VMEM_SPEC),
        scratch_shapes=[
            pltpu.VMEM((4, 8, lanes), F32),
            pltpu.VMEM((3, most, 8, lanes), F32),
            pltpu.SemaphoreType.DMA((3, most)),
            pltpu.SemaphoreType.DMA((3, most)),
        ],
        compiler_params=limits(4 << 20, collective_id=3, has_side_effects=True),
        name="combine",
    )(*(own0, own1, own2, image0, image1, image2))
    out = (4, nx, ny, nz, lanes)
    return answer.reshape(out), left.reshape(out)


def solution(mesh):
    tile = P("gx", "gy", "gz", None)
    field = P(None, "gx", "gy", "gz", None)
    return jax.shard_map(
        on_device,
        mesh=mesh,
        in_specs=(field, tile, tile, tile, tile, tile, P("gx", "gy", "gz"), field),
        out_specs=(field, field),
        check_vma=False,
    )
```

time: 567 us -> 122 us (0.22)
  other arithmetic: 283 us -> 0 us
  blocking collectives: 122 us -> 0 us
  Pallas kernels: 0 us -> 110 us
  matrix products: 78.7 us -> 0 us
  starting transfers between devices: 54.7 us -> 0 us
  waiting for transfers between devices: 9.94 us -> 0 us
    dynamic_update_slice x27 -> x0, other arithmetic: 141 us -> none  [build(): lax.dynamic_update_index_in_dim(store_response, response, offset_code, 0)]
    reduce_sum x38 -> x0, other arithmetic: 136 us -> none  [the longest x27 135 us: build(): row_response = row_response + jnp.sum(response.astype(jnp.float32), axis=2)]
    psum x12 -> x0, blocking collectives: 122 us -> none  [one_axis_at_a_time(): return functools.reduce(lax.psum, axes, shard)]
    pallas_call x0 -> x8, Pallas kernels: none -> 110 us  [the longest x1 33.6 us: on_device(): pl.pallas_call(build, out_shape=(pltpu.VMEM((slots, 2, lanes, lanes), BF)...]
    dot_general x6 -> x0, matrix products: 78.7 us -> none  [the longest x3 39.6 us: operate(): jnp.einsum('otij,oftj->fti', store_coulomb, stacked[:, :4], preferred_ele...]
    ppermute x18 -> x0, starting transfers between devices: 54.7 us -> none  [the longest x9 30.9 us: extended(): lax.ppermute(lax.slice_in_dim(block, block.shape[dim] - width, None, axis...]
    ppermute x18 -> x0, waiting for transfers between devices: 9.94 us -> none  [the longest x9 9.32 us: extended(): lax.ppermute(lax.slice_in_dim(block, block.shape[dim] - width, None, axis...]
    slice x131 -> x0, local copies, waits for them, and re-layouts: 6.94 us -> none  [the longest x87 5 us: static_block(): padded[:, first:first + extent[0], second:second + extent[1], third:third...]
  transfers between devices with their start and end apart: 18 -> 0, of which waited for: 10 -> 0; matrix products, arithmetic and copies ran while one was open for 0% -> 0% of each run, Pallas kernels for 0% -> 0%
where the time goes in v1:
time: 122 us; the launch traced here: 121 us
  Pallas kernels  110 us (90%)
  local copies, waits for them, and re-layouts  10.3 us (8%)
    pallas_call x1, Pallas kernels, on_device(): pl.pallas_call(build, out_shape=(pltpu.VMEM((slots, 2, lanes, lanes), BF)...  33.6 us
    pallas_call x2, Pallas kernels, halo(): pl.pallas_call(next_halo, out_shape=jax.ShapeDtypeStruct(ext + (4, lanes)...  28.5 us
    pallas_call x1, Pallas kernels, on_device(): pl.pallas_call(combine, out_shape=(shape, shape), in_specs=[VMEM_SPEC] *...  19.3 us
    pallas_call x2, Pallas kernels, operate(): pl.pallas_call(again, out_shape=(jax.ShapeDtypeStruct((owned, 4, lanes),...  17.4 us
    pallas_call x1, Pallas kernels, on_device(): pl.pallas_call(lambda pos, sh, wi, rhs, pe, fe, fo, po, ss, rs: first_hal...  11.7 us
    unnamed x32, local copies, waits for them, and re-layouts  8.92 us

profile of v1, /device:TPU:1, one launch (start us, length us, event | category | flops | bytes accessed | tf_op | source)
XLA Modules:
  0.0 121.5 jit_solution(3078526200301511712)
XLA Ops:
  0.6 1.3 %reshape.44.bits = s32[32]{0:T(128)} reshape(s32[2,2,8]{2,1,0:T(2,128)} %param.14) | data formatting | bytes 256 | tf_op jit(solution)/shard_map/reshape | solution.py:497
  2.0 0.0 copy-start.8
  2.0 0.8 copy-done.8
  2.8 0.0 copy-start.12
  2.8 0.8 copy-done.12
  3.6 0.0 copy-start.13
  3.6 0.7 copy-done.13
  4.3 0.0 copy-start.14
  4.3 0.7 copy-done.14
  5.0 11.7 %first_halo.1 = (f32[4,4,10,8,128]{4,3,2,1,0:T(8,128)S(1)}, f32[4,4,10,4,128]{4,3,2,1,0:T(4,128)S(1)}, f32[2,2,8,4,128]{4,3,2,1,0:T(4,128)S(1)}) custom-call(f32[3,2,2,8,128]{4,3,2,1,0:T(8,128)S(1)} %copy-done.12, f32[2,2,8,128]{3,2,1,0:T(8,128)S(1)} %copy-done.13, f32[2,2,8,128]{3,2,1,0:T(8,128)S(1)} %copy-done.14, f32[4,2,2,8,128]{4,3,2,1,0:T(8,128)S(1)} %copy-done.8), custom_call_target="tpu_custom_call" | custom-call | tf_op jit(solution)/shard_map/first_halo/pallas_call | solution.py:447
  16.8 0.0 copy-start.6
  16.8 0.6 copy-done.6
  17.4 33.6 %build.1 = (bf16[864,2,128,128]{3,2,1,0:T(8,128)(2,1)S(1)}, s32[896]{0:T(1024)}, s32[1]{0:T(128)}, f32[32,4,128]{2,1,0:T(4,128)}, f32[32,4,128]{2,1,0:T(4,128)}, /*index=5*/f32[32,4,128]{2,1,0:T(4,128)}) custom-call(s32[32]{0:T(128)} %reshape.44.bits, f32[160,8,128]{2,1,0:T(8,128)S(1)} %bitcast.14, ...), custom_call_target="tpu_custom_call", output_to_operand_aliasing={{0}: (7, {})} | custom-call | tf_op jit(solution)/shard_map/build/pallas_call | solution.py:475
  51.0 0.0 copy-start.2
  51.0 0.8 copy-done.2
  51.8 18.5 %halo.2 = f32[4,4,10,4,128]{4,3,2,1,0:T(4,128)S(1)} custom-call(f32[2,2,8,4,128]{4,3,2,1,0:T(4,128)S(1)} %bitcast.15), custom_call_target="tpu_custom_call" | custom-call | tf_op jit(solution)/shard_map/halo/pallas_call | solution.py:508
  70.3 0.0 copy-start.1
  70.3 0.7 copy-done.1
  71.0 0.0 copy-start.3
  71.0 0.0 copy-start.7
  71.0 0.0 copy-start.9
  71.0 8.7 %apply.2 = (f32[32,4,128]{2,1,0:T(4,128)}, f32[32,4,128]{2,1,0:T(4,128)}, bf16[864,2,128,128]{3,2,1,0:T(8,128)(2,1)S(1)}) custom-call(f32[160,4,128]{2,1,0:T(4,128)} %bitcast.13, f32[32,4,128]{2,1,0:T(4,128)} %get-tuple-element.20.own.u1, f32[4,8,128]{2,1,0:T(8,128)} %bitcast.23, ...), custom_call_target="tpu_custom_call", output_to_operand_aliasing={{2}: (3, {})} | custom-call | tf_op jit(solution)/shard_map/apply/pallas_call | solution.py:520
  79.7 0.0 copy-start.4
  79.7 0.8 copy-done.4
  80.5 0.0 copy-start.5
  80.5 0.0 copy-start.10
  80.5 10.0 %halo.3 = f32[4,4,10,4,128]{4,3,2,1,0:T(4,128)S(1)} custom-call(f32[2,2,8,4,128]{4,3,2,1,0:T(4,128)S(1)} %bitcast.16), custom_call_target="tpu_custom_call" | custom-call | tf_op jit(solution)/shard_map/halo/pallas_call | solution.py:508
  90.6 0.0 copy-start
  90.6 0.7 copy-done
  91.3 8.7 %apply.3 = (f32[32,4,128]{2,1,0:T(4,128)}, f32[32,4,128]{2,1,0:T(4,128)}, bf16[864,2,128,128]{3,2,1,0:T(8,128)(2,1)S(1)}) custom-call(f32[160,4,128]{2,1,0:T(4,128)} %bitcast.12, f32[32,4,128]{2,1,0:T(4,128)} %get-tuple-element.25.own.u2, f32[4,8,128]{2,1,0:T(8,128)} %bitcast.24, ...), custom_call_target="tpu_custom_call", output_to_operand_aliasing={{2}: (3, {})} | custom-call | tf_op jit(solution)/shard_map/apply/pallas_call | solution.py:520
  100.0 0.0 copy-done.3
  100.0 0.0 copy-done.7
  100.0 0.0 copy-done.9
  100.0 0.0 copy-done.5
  100.0 0.0 copy-done.10
  100.0 0.0 copy-start.11
  100.0 0.8 copy-done.11
  100.9 19.3 %combine.1 = (f32[4,4,8,128]{3,2,1,0:T(8,128)S(1)}, f32[4,4,8,128]{3,2,1,0:T(8,128)S(1)}) custom-call(f32[32,4,128]{2,1,0:T(4,128)S(1)} %bitcast.19, f32[32,4,128]{2,1,0:T(4,128)S(1)} %copy-done.3, f32[32,4,128]{2,1,0:T(4,128)S(1)} %copy-done.5, f32[32,4,128]{2,1,0:T(4,128)S(1)} %copy-done.9, f32[32,4,128]{2,1,0:T(4,128)S(1)} %copy-done.10, ...), custom_call_target="tpu_custom_call" | custom-call | tf_op jit(solution)/shard_map/combine/pallas_call | solution.py:543
  120.2 0.6 copy.18
  120.8 0.6 copy.19
  (1 shorter events, 0.0 us)
Async XLA Ops:
  2.0 0.8 copy-start.8
  2.8 0.8 copy-start.12
  3.6 0.7 copy-start.13
  4.3 0.7 copy-start.14
  16.8 0.6 copy-start.6
  51.0 0.8 copy-start.2
  70.3 0.7 copy-start.1
  71.0 29.0 %copy-start.3 = (f32[32,4,128]{2,1,0:T(4,128)S(1)}, f32[32,4,128]{2,1,0:T(4,128)}, u32[]{:S(2)}) copy-start(f32[32,4,128]{2,1,0:T(4,128)} %get-tuple-element.20.own.u1) | copy-start | bytes 196612
  71.0 29.0 %copy-start.7 = (f32[2,2,8,4,128]{4,3,2,1,0:T(4,128)S(1)}, f32[2,2,8,4,128]{4,3,2,1,0:T(4,128)}, u32[]{:S(2)}) copy-start(f32[2,2,8,4,128]{4,3,2,1,0:T(4,128)} %copy-done.6) | copy-start | bytes 196612
  71.0 29.0 %copy-start.9 = (f32[32,4,128]{2,1,0:T(4,128)S(1)}, f32[32,4,128]{2,1,0:T(4,128)}, u32[]{:S(2)}) copy-start(f32[32,4,128]{2,1,0:T(4,128)} %get-tuple-element.26.w0) | copy-start | bytes 196612
  79.7 0.8 copy-start.4
  80.5 19.5 %copy-start.5 = (f32[32,4,128]{2,1,0:T(4,128)S(1)}, f32[32,4,128]{2,1,0:T(4,128)}, u32[]{:S(2)}) copy-start(f32[32,4,128]{2,1,0:T(4,128)} %get-tuple-element.25.own.u2) | copy-start | bytes 196612
  80.5 19.5 %copy-start.10 = (f32[32,4,128]{2,1,0:T(4,128)S(1)}, f32[32,4,128]{2,1,0:T(4,128)}, u32[]{:S(2)}) copy-start(f32[32,4,128]{2,1,0:T(4,128)} %get-tuple-element.27.w1) | copy-start | bytes 196612
  90.6 0.7 copy-start
  100.0 0.8 copy-start.11

commit v2 on v1

--- a/solution.py
+++ b/solution.py
@@ -15,8 +15,8 @@
 LOG2E = 1.4426950408889634
 COULOMB_GAIN = 250000.0
 RESPONSE_SCALE = 0.003
-GROUP = 8
-WIDE = 16
+GROUP = 32
+WIDE = 32
 DIRECTIONS = [d for d in itertools.product((-1, 0, 1), repeat=3) if d != (0, 0, 0)]
 VMEM_SPEC = pl.BlockSpec(memory_space=pltpu.VMEM)
 SMEM_SPEC = pl.BlockSpec(memory_space=pltpu.SMEM)
@@ -98,27 +98,39 @@
                 copy.wait_send()
 
 
-def first_halo(pos, shield, width, rhs, param_ext, field_ext, param_own, field_own, send_sem, recv_sem):
+def first_halo(pos_in, shield_in, width_in, rhs_in, param_ext, field_ext, field_own, *scratch):
+    param_own, last_own, pos, shield, width, rhs, load_sem, send_sem, recv_sem = scratch
+    loads = [
+        pltpu.make_async_copy(source, target, load_sem.at[index])
+        for index, (source, target) in enumerate(
+            ((pos_in, pos), (shield_in, shield), (width_in, width), (rhs_in, rhs))
+        )
+    ]
+    for load in loads:
+        load.start()
     param_ext[...] = jnp.zeros_like(param_ext)
     field_ext[...] = jnp.zeros_like(field_ext)
     barrier, count = greet()
-    nx, ny, nz = shield.shape[:3]
+    for load in loads:
+        load.wait()
+    nx, ny, nz = param_own.shape[:3]
     for x in range(nx):
         for y in range(ny):
             columns = [pos[0, x, y], pos[1, x, y], pos[2, x, y], shield[x, y], width[x, y]]
-            fields = [rhs[f, x, y] for f in range(4)]
+            columns = columns + [rhs[f, x, y] for f in range(4)]
             for z in range(nz):
-                for f in range(5):
+                for f in range(9):
                     row = columns[f][z : z + 1]
-                    param_own[x, y, z, f : f + 1, :] = row
-                    param_ext[x + 1, y + 1, z + 1, f : f + 1, :] = row
-                param_own[x, y, z, 5:8, :] = jnp.zeros((3, 128), F32)
-                for f in range(4):
-                    row = fields[f][z : z + 1]
-                    field_own[x, y, z, f : f + 1, :] = row
-                    field_ext[x + 1, y + 1, z + 1, f : f + 1, :] = row
+                    if f < 8:
+                        param_own[x, y, z, f : f + 1, :] = row
+                        param_ext[x + 1, y + 1, z + 1, f : f + 1, :] = row
+                    else:
+                        last_own[x, y, z] = row
+                        field_ext[x + 1, y + 1, z + 1] = row
+                    if f > 4:
+                        field_own[x, y, z, f - 5 : f - 4, :] = row
     pl.semaphore_wait(barrier, count)
-    exchange(((param_own, param_ext), (field_own, field_ext)), send_sem, recv_sem)
+    exchange(((param_own, param_ext), (last_own, field_ext)), send_sem, recv_sem)
 
 
 def next_halo(own, ext, send_sem, recv_sem):
@@ -174,114 +186,113 @@
     return jnp.concatenate(sides, axis=1)
 
 
-def split_fields(ext, halves, tiles):
+def split_fields(load, halves, tiles):
     ones = jnp.ones((8, 128), F32)
 
     def step(index, carry):
-        for sub in range(8):
-            e = index * 8 + sub
-            value = ext[e]
+        values = [load(index * 16 + sub) for sub in range(16)]
+        parts = []
+        for value in values:
             high = value.astype(BF).astype(F32)
-            low = value - high
-            halves[e] = jnp.concatenate([high, low, ones], axis=0).astype(BF)
+            parts.append(jnp.concatenate([high, value - high, ones], axis=0).astype(BF))
+        for sub in range(16):
+            halves[index * 16 + sub] = parts[sub]
         return carry
 
-    lax.fori_loop(0, tiles // 8, step, 0)
-
-
-def apply_pairs(groups, entries, halves, store, acc):
-    acc[...] = jnp.zeros_like(acc)
-
-    def step(index, carry):
-        for sub in range(WIDE):
-            slot = index * WIDE + sub
-            code = entries[slot]
-            e = code & 255
-            t = lax.shift_right_logical(code, 16)
-            both = jnp.concatenate([store[slot, 0], store[slot, 1]], axis=1)
-            out = jnp.dot(halves[e], both, preferred_element_type=F32)
-            acc[t] = acc[t] + out
-        return carry
-
-    lax.fori_loop(0, groups, step, 0)
-
-
-def diagonal_image(t, out, diagonal, coupling, vector):
+    lax.fori_loop(0, tiles // 16, step, 0)
+
+
+def apply_group(base, size, entries, halves, window, acc):
+    rows = acc.shape[1]
+    for sub in range(size):
+        code = entries[base + sub]
+        e = code & 255
+        t = lax.shift_right_logical(code, 16)
+        both = jnp.concatenate([window[sub, 0], window[sub, 1]], axis=1)
+        out = jnp.dot(halves[e], both, preferred_element_type=F32)
+        acc[t] = acc[t] + out[:rows]
+
+
+def image_rows(out, diagonal, link, value):
     row = lax.broadcasted_iota(jnp.int32, (4, 128), 0)
     summed = out[0:4] + out[4:8]
     pair = jnp.where(row < 2, summed[:, :128], -summed[:, 128:])
-    value = vector[t]
     swapped = jnp.concatenate([value[2:4], value[0:2]], axis=0)
-    return diagonal * value + pair + coupling[t // 8, pl.ds(t % 8, 1), :] * swapped
+    return diagonal * value + pair + link * swapped
+
+
+def finish_all(owned, make):
+    def step(index, carry):
+        results = [make(index, sub) for sub in range(8)]
+        for sub, (targets, values) in enumerate(results):
+            for target, value in zip(targets, values):
+                target[index * 8 + sub] = value
+        return carry
+
+    lax.fori_loop(0, owned // 8, step, 0)
 
 
 def build(
     bits, param, field, own, hardness, softness, coupling, blank, store, entries, count, diagonal, image, send,
     features, mine, halves, acc
 ):
-    ex_size, ey_size, ez_size = 4, 4, 10
+    ey_size, ez_size = 4, 10
     half = (2.0, 2.0, 5.0)
-    tiles = ex_size * ey_size * ez_size
+    tiles = 160
     owned = 32
 
-    def features_step(index, carry):
-        for sub in range(4):
-            e = index * 4 + sub
-            ex = e // (ey_size * ez_size)
-            ey = (e // ez_size) % ey_size
-            ez = e % ez_size
-            rows = partner_features(param[e], ex, ey, ez, half)
-            features[e, :, 0:48] = rows.T.astype(BF)
-        return carry
-
-    lax.fori_loop(0, tiles // 4, features_step, 0)
-
-    def own_step(index, carry):
+    def place_of(t):
+        return ((t // 16 + 1) * ey_size + t // 8 % 2 + 1) * ez_size + t % 8 + 1
+
+    def features_step(index, at):
+        ex = lax.shift_right_logical(index, 2)
+        ey = index & 3
+        loaded = [param[index * ez_size + ez] for ez in range(ez_size)]
+        made = [partner_features(loaded[ez], ex, ey, ez, half).T.astype(BF) for ez in range(ez_size)]
+        for ez in range(ez_size):
+            features[index * ez_size + ez, :, 0:48] = made[ez]
         for sub in range(2):
             t = index * 2 + sub
-            ex = t // 16 + 1
-            ey = (t // 8) % 2 + 1
-            ez = t % 8 + 1
-            e = (ex * ey_size + ey) * ez_size + ez
-            mine[t] = own_features(param[e], ex, ey, ez, half).astype(BF)
-            entries[t] = e + 256 * t + 65536 * t
-        return carry
-
-    lax.fori_loop(0, owned // 2, own_step, 0)
-    split_fields(field, halves, tiles)
-
-    def list_step(t, at):
-        ex = t // 16 + 1
-        ey = (t // 8) % 2 + 1
-        ez = t % 8 + 1
-        e = (ex * ey_size + ey) * ez_size + ez
-        word = bits[t]
-        for code in range(27):
-            if code == 13:
-                continue
-            shift = ((code // 9 - 1) * ey_size + (code // 3 % 3 - 1)) * ez_size + code % 3 - 1
-            entries[at] = (e + shift) + 256 * t + 65536 * t
-            at = at + (lax.shift_right_logical(word, code) & 1)
+            x = lax.shift_right_logical(t, 4)
+            y = lax.shift_right_logical(t, 3) & 1
+            z = t & 7
+            word = bits[x, y, z]
+            own_code = ((x + 1) * ey_size + y + 1) * ez_size + z + 1 + 65792 * t
+            entries[t] = own_code
+            for code in range(27):
+                if code == 13:
+                    continue
+                shift = ((code // 9 - 1) * ey_size + (code // 3 % 3 - 1)) * ez_size + code % 3 - 1
+                entries[at] = own_code + shift
+                at = at + (lax.shift_right_logical(word, code) & 1)
         return at
 
-    total = lax.fori_loop(0, owned, list_step, jnp.int32(owned))
+    total = lax.fori_loop(0, 16, features_step, jnp.int32(owned))
     middle = (ey_size + 1) * ez_size + 1
     for sub in range(WIDE):
         entries[total + sub] = middle + 65536 * owned
     count[0] = total
 
-    def pair(slot, masked):
+    def own_step(index, carry):
+        ex = lax.shift_right_logical(index, 1) + 1
+        ey = (index & 1) + 1
+        first = (ex * ey_size + ey) * ez_size + 1
+        made = [own_features(param[first + z], ex, ey, z + 1, half).astype(BF) for z in range(8)]
+        for z in range(8):
+            mine[index * 8 + z] = made[z]
+        return carry
+
+    lax.fori_loop(0, owned // 8, own_step, 0)
+    split_fields(lambda e: jnp.concatenate([param[e, 5:8, :], field[e]], axis=0), halves, tiles)
+    acc[...] = jnp.zeros_like(acc)
+
+    def pair(slot, window, sub, masked):
         code = entries[slot]
         e = code & 255
         t = lax.shift_right_logical(code, 8) & 255
         both = jnp.dot(features[e, :, 0:48], mine[t], preferred_element_type=F32)
-        width_row = param[e, 4:5, :]
-        partner_width = jnp.broadcast_to(width_row, (128, 128)).T
-        ex = t // 16 + 1
-        ey = (t // 8) % 2 + 1
-        ez = t % 8 + 1
-        here = (ex * ey_size + ey) * ez_size + ez
-        widths = partner_width + param[here, 4:5, :]
+        partner_width = jnp.broadcast_to(param[e, 4:5, :], (128, 128)).T
+        widths = partner_width + param[place_of(t), 4:5, :]
         coulomb = lax.rsqrt(both[:, 128:])
         response = RESPONSE_SCALE * jnp.exp2(both[:, :128] / widths)
         if masked:
@@ -290,125 +301,110 @@
             )
             coulomb = jnp.where(same, 0.0, coulomb)
             response = jnp.where(same, 0.0, response)
-        store[slot, 0] = coulomb.astype(BF)
-        store[slot, 1] = response.astype(BF)
+        window[sub, 0] = coulomb.astype(BF)
+        window[sub, 1] = response.astype(BF)
 
     def self_step(index, carry):
-        for sub in range(4):
-            pair(index * 4 + sub, True)
+        window = store.at[pl.ds(index * 8, 8)]
+        for sub in range(8):
+            pair(index * 8 + sub, window, sub, True)
         return carry
 
-    lax.fori_loop(0, owned // 4, self_step, 0)
+    lax.fori_loop(0, owned // 8, self_step, 0)
+    apply_group(0, owned - GROUP, entries, halves, store, acc)
 
     def pair_step(index, carry):
+        base = owned + index * GROUP
+        window = store.at[pl.ds(base - GROUP, 2 * GROUP)]
+        apply_group(base - GROUP, GROUP, entries, halves, window, acc)
         for sub in range(GROUP):
-            pair(owned + index * GROUP + sub, False)
+            pair(base + sub, window, GROUP + sub, False)
         return carry
 
-    lax.fori_loop(0, (total - owned + GROUP - 1) // GROUP, pair_step, 0)
-    apply_pairs((total + WIDE - 1) // WIDE, entries, halves, store, acc)
-
+    groups = (total - owned + GROUP - 1) // GROUP
+    lax.fori_loop(0, groups, pair_step, 0)
+    last = owned + (groups - 1) * GROUP
+    apply_group(last, GROUP, entries, halves, store.at[pl.ds(last, GROUP)], acc)
     row = lax.broadcasted_iota(jnp.int32, (4, 128), 0)
 
-    def finish(t, carry):
-        out = acc[t]
-        a, b = t // 8, pl.ds(t % 8, 1)
-        top = hardness[a, b, :] + out[8:9, :128]
-        low = softness[a, b, :] + out[8:9, 128:]
+    def make(index, sub):
+        out = acc[index * 8 + sub]
+        value = own[index * 8 + sub]
+        top = hardness[index, sub : sub + 1, :] + out[8:9, :128]
+        low = softness[index, sub : sub + 1, :] + out[8:9, 128:]
         diag = jnp.where(row < 2, top, low)
-        diagonal[t] = diag
-        value = diagonal_image(t, out, diag, coupling, own)
-        image[t] = value
-        send[t] = value - SHIFT * own[t]
-        return carry
-
-    lax.fori_loop(0, owned, finish, 0)
+        made = image_rows(out, diag, coupling[index, sub : sub + 1, :], value)
+        return (diagonal, image, send), (diag, made, made - SHIFT * value)
+
+    finish_all(owned, make)
 
 
 def again(field, own, coupling, store, entries, count, diagonal, image, send, passed, halves, acc):
     owned = 32
-    split_fields(field, halves, field.shape[0])
-    apply_pairs((count[0] + WIDE - 1) // WIDE, entries, halves, store, acc)
-
-    def finish(t, carry):
-        value = diagonal_image(t, acc[t], diagonal[t], coupling, own)
-        image[t] = value
-        send[t] = value - SHIFT * own[t]
+    split_fields(lambda e: field[e], halves, field.shape[0])
+    acc[...] = jnp.zeros_like(acc)
+
+    def step(index, carry):
+        apply_group(index * WIDE, WIDE, entries, halves, store.at[pl.ds(index * WIDE, WIDE)], acc)
         return carry
 
-    lax.fori_loop(0, owned, finish, 0)
-
-
-def combine(u0, u1, u2, w0, w1, w2, solution, residual, part, stage, send_sem, recv_sem):
-    basis = (u0, u1, u2)
-    images = (w0, w1, w2)
+    lax.fori_loop(0, (count[0] + WIDE - 1) // WIDE, step, 0)
+
+    def make(index, sub):
+        value = own[index * 8 + sub]
+        diag = diagonal[index * 8 + sub]
+        made = image_rows(acc[index * 8 + sub], diag, coupling[index, sub : sub + 1, :], value)
+        return (image, send), (made, made - SHIFT * value)
+
+    finish_all(owned, make)
+
+
+def combine(u0, u1, u2, w0, w1, w2, solution, residual, part, plane, line, send_sem, recv_sem):
     sizes = [lax.axis_size(axis) for axis in AXES]
-    places = [lax.axis_index(axis) for axis in AXES]
+    gx, gy, gz = (lax.axis_index(axis) for axis in AXES)
+    across = []
+    for a in range(sizes[1]):
+        for b in range(sizes[2]):
+            if a or b:
+                across.append((gx, lax.rem(gy + a, sizes[1]), lax.rem(gz + b, sizes[2])))
+    along = [(lax.rem(gx + a, sizes[0]), gy, gz) for a in range(1, sizes[0])]
     barrier = pltpu.get_barrier_semaphore()
-    for which, size in enumerate(sizes):
-        for step in range(1, size):
-            peer = list(places)
-            peer[which] = lax.rem(places[which] + step, size)
-            pl.semaphore_signal(barrier, inc=1, device_id=tuple(peer), device_id_type=MESH)
+    for peer in across + along:
+        pl.semaphore_signal(barrier, inc=1, device_id=peer, device_id_type=MESH)
 
     wanted = [(u0, u0), (u0, u1), (u0, u2), (u0, w0), (u0, w1), (u0, w2), (u1, w1), (u1, w2), (u2, w2)]
     sums = []
     for left, right in wanted:
         both = jnp.sum(left[...] * right[...], axis=0)
         sums.append(both[0:2] + both[2:4])
-    lane = lax.broadcasted_iota(jnp.int32, (8, 128), 1)
-    packed = jnp.zeros((8, 128), F32)
-    for block in range(3):
-        rows = sums[4 * block : 4 * block + 4]
-        rows = rows + [jnp.zeros((2, 128), F32)] * (4 - len(rows))
-        folded = jnp.concatenate(rows, axis=0)
-        folded = folded + pltpu.roll(folded, 64, 1)
-        folded = folded + pltpu.roll(folded, 32, 1)
-        packed = jnp.where((lane >= 32 * block) & (lane < 32 * block + 32), folded, packed)
-    part[0] = packed
-    pl.semaphore_wait(barrier, sum(size - 1 for size in sizes))
-
-    for turn, which in enumerate((2, 1, 0)):
-        size = sizes[which]
+    stacked = jnp.concatenate(sums + [jnp.zeros((128 - 18, 128), F32)], axis=0)
+    part[0] = jnp.sum(stacked.T, axis=0, keepdims=True)
+    pl.semaphore_wait(barrier, len(across) + len(along))
+
+    def gather(turn, peers, here, stage, width):
         made = []
-        for step in range(1, size):
-            peer = list(places)
-            peer[which] = lax.rem(places[which] + step, size)
+        for index, peer in enumerate(peers):
             copy = pltpu.make_async_remote_copy(
                 part.at[turn],
-                stage.at[turn, step - 1],
-                send_sem.at[turn, step - 1],
-                recv_sem.at[turn, step - 1],
-                device_id=tuple(peer),
+                stage.at[here],
+                send_sem.at[turn, index],
+                recv_sem.at[turn, index],
+                device_id=peer,
                 device_id_type=MESH,
             )
             copy.start()
             made.append(copy)
-        mine = part[turn]
+        stage[here] = part[turn]
         for copy in made:
             copy.wait_recv()
-        received = [mine] + [stage[turn, step - 1] for step in range(1, size)]
-        total = jnp.zeros((8, 128), F32)
-        for place in range(size):
-            term = jnp.zeros((8, 128), F32)
-            for step in range(size):
-                term = jnp.where(lax.rem(places[which] - step + size, size) == place, received[step], term)
-            total = total + term
+        total = jnp.sum(stage[...], axis=0)
         for copy in made:
             copy.wait_send()
-        part[turn + 1] = total
-
-    total = part[3]
-    gram = {}
-    values = []
-    for block in range(3):
-        inside = (lane >= 32 * block) & (lane < 32 * block + 32)
-        values.append(jnp.sum(jnp.where(inside, total, 0.0), axis=1, keepdims=True))
-    value = []
-    for index in range(9):
-        two = values[index // 4][2 * (index % 4) : 2 * (index % 4) + 2]
-        value.append(jnp.concatenate([two, two], axis=0))
-    m0, m1, m2, g00, g01, g02, g11, g12, g22 = value
+        return total
+
+    part[1] = gather(0, across, gy * sizes[2] + gz, plane, len(across) + 1)
+    total = gather(1, along, gx, line, len(along) + 1)
+    m0, m1, m2, g00, g01, g02, g11, g12, g22 = (total[:, 2 * k : 2 * k + 2] for k in range(9))
     f1 = g01 / g00
     f2 = g02 / g00
     h11 = g11 - f1 * g01
@@ -422,7 +418,12 @@
     c2 = k2 / k22
     c1 = (n1 - h12 * c2) / h11
     c0 = (m0 - g01 * c1 - g02 * c2) / g00
-    c0, c1, c2 = (jnp.broadcast_to(c, (4, 128))[None] for c in (c0, c1, c2))
+
+    def spread(c):
+        pair = [jnp.broadcast_to(c[:, r : r + 1], (1, 128)) for r in range(2)]
+        return jnp.concatenate(pair + pair, axis=0)[None]
+
+    c0, c1, c2 = (spread(c) for c in (c0, c1, c2))
     answer = c0 * u0[...] + c1 * u1[...] + c2 * u2[...]
     left = u0[...] - (c0 * w0[...] + c1 * w1[...] + c2 * w2[...])
     for t in range(32):
@@ -445,16 +446,22 @@
         return pltpu.CompilerParams(vmem_limit_bytes=size, **more)
 
     param_ext, field_ext, field_own = pl.pallas_call(
-        lambda pos, sh, wi, rhs, pe, fe, fo, po, ss, rs: first_halo(pos, sh, wi, rhs, pe, fe, po, fo, ss, rs),
+        first_halo,
         out_shape=(
             pltpu.VMEM(ext + (8, lanes), F32),
-            pltpu.VMEM(ext + (4, lanes), F32),
+            pltpu.VMEM(ext + (1, lanes), F32),
             pltpu.VMEM((nx, ny, nz, 4, lanes), F32),
         ),
-        in_specs=[VMEM_SPEC] * 4,
+        in_specs=[pl.BlockSpec(memory_space=pltpu.HBM)] * 4,
         out_specs=(VMEM_SPEC,) * 3,
         scratch_shapes=[
             pltpu.VMEM((nx, ny, nz, 8, lanes), F32),
+            pltpu.VMEM((nx, ny, nz, 1, lanes), F32),
+            pltpu.VMEM(positions.shape, F32),
+            pltpu.VMEM(shield.shape, F32),
+            pltpu.VMEM(width.shape, F32),
+            pltpu.VMEM(right_side.shape, F32),
+            pltpu.SemaphoreType.DMA((4,)),
             pltpu.SemaphoreType.DMA((2, 26)),
             pltpu.SemaphoreType.DMA((2, 26)),
         ],
@@ -494,9 +501,9 @@
         compiler_params=limits(8 << 20),
         name="build",
     )(
-        pair_bits.reshape(owned),
+        pair_bits,
         kept(param_ext.reshape(tiles, 8, lanes)),
-        kept(field_ext.reshape(tiles, 4, lanes)),
+        kept(field_ext.reshape(tiles, 1, lanes)),
         own0,
         hard,
         soft,
@@ -529,7 +536,7 @@
             input_output_aliases={3: 2},
             scratch_shapes=[
                 pltpu.VMEM((tiles, 16, lanes), BF),
-                pltpu.VMEM((owned + 1, 16, 2 * lanes), F32),
+                pltpu.VMEM((owned + 1, 8, 2 * lanes), F32),
             ],
             compiler_params=limits(4 << 20),
             name="apply",
@@ -537,8 +544,8 @@
 
     image1, own2, store = operate(own1, store, 1)
     image2, _, _ = operate(own2, store, 2)
-    sizes = [lax.axis_size(axis) for axis in AXES]
-    most = max(sizes) - 1
+    line = lax.axis_size("gx")
+    plane = lax.axis_size("gy") * lax.axis_size("gz")
     shape = jax.ShapeDtypeStruct((4, owned // 8, 8, lanes), F32)
     answer, left = pl.pallas_call(
         combine,
@@ -546,10 +553,11 @@
         in_specs=[VMEM_SPEC] * 6,
         out_specs=(VMEM_SPEC, VMEM_SPEC),
         scratch_shapes=[
-            pltpu.VMEM((4, 8, lanes), F32),
-            pltpu.VMEM((3, most, 8, lanes), F32),
-            pltpu.SemaphoreType.DMA((3, most)),
-            pltpu.SemaphoreType.DMA((3, most)),
+            pltpu.VMEM((2, 1, lanes), F32),
+            pltpu.VMEM((plane, 1, lanes), F32),
+            pltpu.VMEM((line, 1, lanes), F32),
+            pltpu.SemaphoreType.DMA((2, plane - 1)),
+            pltpu.SemaphoreType.DMA((2, plane - 1)),
         ],
         compiler_params=limits(4 << 20, collective_id=3, has_side_effects=True),
         name="combine",

time: 122 us -> 99.5 us (0.82)
  Pallas kernels: 110 us -> 89.5 us
  local copies, waits for them, and re-layouts: 10.3 us -> 8.91 us
    pallas_call x1, Pallas kernels: 33.6 us -> 21.4 us  [on_device(): pl.pallas_call(build, out_shape=(pltpu.VMEM((slots, 2, lanes, lanes), BF)...]
    pallas_call x2, Pallas kernels: 28.5 us -> 23.4 us  [halo(): pl.pallas_call(next_halo, out_shape=jax.ShapeDtypeStruct(ext + (4, lanes)...]
    pallas_call x2, Pallas kernels: 17.4 us -> 15.1 us  [operate(): pl.pallas_call(again, out_shape=(jax.ShapeDtypeStruct((owned, 4, lanes),...]
    reshape x1 -> x0, local copies, waits for them, and re-layouts: 1.34 us -> none  [on_device(): pair_bits.reshape(owned)]
where the time goes in v2:
time: 99.5 us; the launch traced here: 99.2 us
  Pallas kernels  89.5 us (90%)
  local copies, waits for them, and re-layouts  8.91 us (9%)
    pallas_call x2, Pallas kernels, halo(): pl.pallas_call(next_halo, out_shape=jax.ShapeDtypeStruct(ext + (4, lanes)...  23.4 us
    pallas_call x1, Pallas kernels, on_device(): pl.pallas_call(build, out_shape=(pltpu.VMEM((slots, 2, lanes, lanes), BF)...  21.4 us
    pallas_call x1, Pallas kernels, on_device(): pl.pallas_call(combine, out_shape=(shape, shape), in_specs=[VMEM_SPEC] *...  18.6 us
    pallas_call x2, Pallas kernels, operate(): pl.pallas_call(again, out_shape=(jax.ShapeDtypeStruct((owned, 4, lanes),...  15.1 us
    pallas_call x1, Pallas kernels, on_device(): pl.pallas_call(first_halo, out_shape=(pltpu.VMEM(ext + (8, lanes), F32),...  11.1 us
    unnamed x32, local copies, waits for them, and re-layouts  8.91 us

profile of v2, /device:TPU:1, one launch (start us, length us, event | category | flops | bytes accessed | tf_op | source)
XLA Modules:
  0.0 99.2 jit_solution(10928772315066612431)
XLA Ops:
  0.6 0.0 copy-start.8
  0.6 0.8 copy-done.8
  1.5 0.0 copy-start.12
  1.5 0.8 copy-done.12
  2.3 0.0 copy-start.13
  2.3 0.7 copy-done.13
  3.0 0.0 copy-start.14
  3.0 0.7 copy-done.14
  3.7 11.1 %first_halo.1 = (f32[4,4,10,8,128]{4,3,2,1,0:T(8,128)S(1)}, f32[4,4,10,1,128]{4,3,2,1,0:T(1,128)S(1)}, f32[2,2,8,4,128]{4,3,2,1,0:T(4,128)S(1)}) custom-call(f32[3,2,2,8,128]{4,3,2,1,0:T(8,128)S(1)} %copy-done.12, f32[2,2,8,128]{3,2,1,0:T(8,128)S(1)} %copy-done.13, f32[2,2,8,128]{3,2,1,0:T(8,128)S(1)} %copy-done.14, f32[4,2,2,8,128]{4,3,2,1,0:T(8,128)S(1)} %copy-done.8), custom_call_target="tpu_custom_call" | custom-call | tf_op jit(solution)/shard_map/first_halo/pallas_call | solution.py:448
  14.8 0.0 copy-start.6
  14.8 0.6 copy-done.6
  15.4 21.4 %build.1 = (bf16[864,2,128,128]{3,2,1,0:T(8,128)(2,1)S(1)}, s32[896]{0:T(1024)}, s32[1]{0:T(128)}, f32[32,4,128]{2,1,0:T(4,128)}, f32[32,4,128]{2,1,0:T(4,128)}, /*index=5*/f32[32,4,128]{2,1,0:T(4,128)}) custom-call(s32[2,2,8]{2,1,0:T(2,128)} %bits.1, f32[160,8,128]{2,1,0:T(8,128)S(1)} %bitcast.14, ...), custom_call_target="tpu_custom_call", output_to_operand_aliasing={{0}: (7, {})} | custom-call | tf_op jit(solution)/shard_map/build/pallas_call | solution.py:482
  36.8 0.0 copy-start.2
  36.8 0.8 copy-done.2
  37.7 14.5 %halo.2 = f32[4,4,10,4,128]{4,3,2,1,0:T(4,128)S(1)} custom-call(f32[2,2,8,4,128]{4,3,2,1,0:T(4,128)S(1)} %bitcast.15), custom_call_target="tpu_custom_call" | custom-call | tf_op jit(solution)/shard_map/halo/pallas_call | solution.py:515
  52.1 0.0 copy-start.1
  52.1 0.7 copy-done.1
  52.9 0.0 copy-start.3
  52.9 0.0 copy-start.7
  52.9 0.0 copy-start.9
  52.9 7.6 %apply.2 = (f32[32,4,128]{2,1,0:T(4,128)}, f32[32,4,128]{2,1,0:T(4,128)}, bf16[864,2,128,128]{3,2,1,0:T(8,128)(2,1)S(1)}) custom-call(f32[160,4,128]{2,1,0:T(4,128)} %bitcast.13, f32[32,4,128]{2,1,0:T(4,128)} %get-tuple-element.20.own.u1, f32[4,8,128]{2,1,0:T(8,128)} %bitcast.23, ...), custom_call_target="tpu_custom_call", output_to_operand_aliasing={{2}: (3, {})} | custom-call | tf_op jit(solution)/shard_map/apply/pallas_call | solution.py:527
  60.4 0.0 copy-start.4
  60.4 0.8 copy-done.4
  61.3 0.0 copy-start.5
  61.3 0.0 copy-start.10
  61.3 8.9 %halo.3 = f32[4,4,10,4,128]{4,3,2,1,0:T(4,128)S(1)} custom-call(f32[2,2,8,4,128]{4,3,2,1,0:T(4,128)S(1)} %bitcast.16), custom_call_target="tpu_custom_call" | custom-call | tf_op jit(solution)/shard_map/halo/pallas_call | solution.py:515
  70.2 0.0 copy-start
  70.2 0.7 copy-done
  70.9 7.5 %apply.3 = (f32[32,4,128]{2,1,0:T(4,128)}, f32[32,4,128]{2,1,0:T(4,128)}, bf16[864,2,128,128]{3,2,1,0:T(8,128)(2,1)S(1)}) custom-call(f32[160,4,128]{2,1,0:T(4,128)} %bitcast.12, f32[32,4,128]{2,1,0:T(4,128)} %get-tuple-element.25.own.u2, f32[4,8,128]{2,1,0:T(8,128)} %bitcast.24, ...), custom_call_target="tpu_custom_call", output_to_operand_aliasing={{2}: (3, {})} | custom-call | tf_op jit(solution)/shard_map/apply/pallas_call | solution.py:527
  78.5 0.0 copy-done.3
  78.5 0.0 copy-done.7
  78.5 0.0 copy-done.9
  78.5 0.0 copy-done.5
  78.5 0.0 copy-done.10
  78.5 0.0 copy-start.11
  78.5 0.8 copy-done.11
  79.3 18.6 %combine.1 = (f32[4,4,8,128]{3,2,1,0:T(8,128)S(1)}, f32[4,4,8,128]{3,2,1,0:T(8,128)S(1)}) custom-call(f32[32,4,128]{2,1,0:T(4,128)S(1)} %bitcast.18, f32[32,4,128]{2,1,0:T(4,128)S(1)} %copy-done.3, f32[32,4,128]{2,1,0:T(4,128)S(1)} %copy-done.5, f32[32,4,128]{2,1,0:T(4,128)S(1)} %copy-done.9, f32[32,4,128]{2,1,0:T(4,128)S(1)} %copy-done.10, ...), custom_call_target="tpu_custom_call" | custom-call | tf_op jit(solution)/shard_map/combine/pallas_call | solution.py:550
  97.9 0.6 copy.18
  98.5 0.6 copy.19
  (1 shorter events, 0.0 us)
Async XLA Ops:
  0.6 0.8 copy-start.8
  1.5 0.8 copy-start.12
  2.3 0.7 copy-start.13
  3.0 0.7 copy-start.14
  14.8 0.6 copy-start.6
  36.8 0.8 copy-start.2
  52.1 0.7 copy-start.1
  52.9 25.6 %copy-start.3 = (f32[32,4,128]{2,1,0:T(4,128)S(1)}, f32[32,4,128]{2,1,0:T(4,128)}, u32[]{:S(2)}) copy-start(f32[32,4,128]{2,1,0:T(4,128)} %get-tuple-element.20.own.u1) | copy-start | bytes 196612
  52.9 25.6 %copy-start.7 = (f32[2,2,8,4,128]{4,3,2,1,0:T(4,128)S(1)}, f32[2,2,8,4,128]{4,3,2,1,0:T(4,128)}, u32[]{:S(2)}) copy-start(f32[2,2,8,4,128]{4,3,2,1,0:T(4,128)} %copy-done.6) | copy-start | bytes 196612
  52.9 25.6 %copy-start.9 = (f32[32,4,128]{2,1,0:T(4,128)S(1)}, f32[32,4,128]{2,1,0:T(4,128)}, u32[]{:S(2)}) copy-start(f32[32,4,128]{2,1,0:T(4,128)} %get-tuple-element.26.w0) | copy-start | bytes 196612
  60.4 0.8 copy-start.4
  61.3 17.2 %copy-start.5 = (f32[32,4,128]{2,1,0:T(4,128)S(1)}, f32[32,4,128]{2,1,0:T(4,128)}, u32[]{:S(2)}) copy-start(f32[32,4,128]{2,1,0:T(4,128)} %get-tuple-element.25.own.u2) | copy-start | bytes 196612
  61.3 17.2 %copy-start.10 = (f32[32,4,128]{2,1,0:T(4,128)S(1)}, f32[32,4,128]{2,1,0:T(4,128)}, u32[]{:S(2)}) copy-start(f32[32,4,128]{2,1,0:T(4,128)} %get-tuple-element.27.w1) | copy-start | bytes 196612
  70.2 0.7 copy-start
  78.5 0.8 copy-start.11

commit v3 on v2

--- a/solution.py
+++ b/solution.py
@@ -98,7 +98,7 @@
                 copy.wait_send()
 
 
-def first_halo(pos_in, shield_in, width_in, rhs_in, param_ext, field_ext, field_own, *scratch):
+def first_halo(pos_in, shield_in, width_in, rhs_in, param_ext, field_ext, *scratch):
     param_own, last_own, pos, shield, width, rhs, load_sem, send_sem, recv_sem = scratch
     loads = [
         pltpu.make_async_copy(source, target, load_sem.at[index])
@@ -127,8 +127,6 @@
                     else:
                         last_own[x, y, z] = row
                         field_ext[x + 1, y + 1, z + 1] = row
-                    if f > 4:
-                        field_own[x, y, z, f - 5 : f - 4, :] = row
     pl.semaphore_wait(barrier, count)
     exchange(((param_own, param_ext), (last_own, field_ext)), send_sem, recv_sem)
 
@@ -233,7 +231,7 @@
 
 
 def build(
-    bits, param, field, own, hardness, softness, coupling, blank, store, entries, count, diagonal, image, send,
+    bits, param, field, hardness, softness, coupling, blank, store, entries, count, diagonal, image, own, send,
     features, mine, halves, acc
 ):
     ey_size, ez_size = 4, 10
@@ -329,17 +327,18 @@
 
     def make(index, sub):
         out = acc[index * 8 + sub]
-        value = own[index * 8 + sub]
+        e = place_of(index * 8) + sub
+        value = jnp.concatenate([param[e, 5:8, :], field[e]], axis=0)
         top = hardness[index, sub : sub + 1, :] + out[8:9, :128]
         low = softness[index, sub : sub + 1, :] + out[8:9, 128:]
         diag = jnp.where(row < 2, top, low)
         made = image_rows(out, diag, coupling[index, sub : sub + 1, :], value)
-        return (diagonal, image, send), (diag, made, made - SHIFT * value)
+        return (diagonal, image, own, send), (diag, made, value, made - SHIFT * value)
 
     finish_all(owned, make)
 
 
-def again(field, own, coupling, store, entries, count, diagonal, image, send, passed, halves, acc):
+def again(field, own, coupling, store, entries, count, diagonal, unused, idle, image, send, passed, halves, acc):
     owned = 32
     split_fields(lambda e: field[e], halves, field.shape[0])
     acc[...] = jnp.zeros_like(acc)
@@ -442,18 +441,20 @@
     def kept(value):
         return pltpu.with_memory_space_constraint(value, pltpu.VMEM)
 
+    def far(value):
+        return pltpu.with_memory_space_constraint(value, pltpu.HBM)
+
     def limits(size, **more):
         return pltpu.CompilerParams(vmem_limit_bytes=size, **more)
 
-    param_ext, field_ext, field_own = pl.pallas_call(
+    param_ext, field_ext = pl.pallas_call(
         first_halo,
         out_shape=(
             pltpu.VMEM(ext + (8, lanes), F32),
             pltpu.VMEM(ext + (1, lanes), F32),
-            pltpu.VMEM((nx, ny, nz, 4, lanes), F32),
         ),
         in_specs=[pl.BlockSpec(memory_space=pltpu.HBM)] * 4,
-        out_specs=(VMEM_SPEC,) * 3,
+        out_specs=(VMEM_SPEC,) * 2,
         scratch_shapes=[
             pltpu.VMEM((nx, ny, nz, 8, lanes), F32),
             pltpu.VMEM((nx, ny, nz, 1, lanes), F32),
@@ -467,31 +468,31 @@
         ],
         compiler_params=limits(4 << 20, collective_id=0, has_side_effects=True),
         name="first_halo",
-    )(positions, shield, width, right_side)
+    )(*(far(a) for a in (positions, shield, width, right_side)))
 
     hard, soft, link = (a.reshape(owned // 8, 8, lanes) for a in (hardness, softness, coupling))
-    own0 = field_own.reshape(owned, 4, lanes)
     vector = jax.ShapeDtypeStruct((owned, 4, lanes), F32)
     blank = pl.pallas_call(
         lambda ref: None,
         out_shape=pltpu.VMEM((slots, 2, lanes, lanes), BF),
         out_specs=VMEM_SPEC,
-        compiler_params=limits(1 << 20),
+        compiler_params=limits(8 << 20),
         name="reserve",
     )()
-    store, entries, count, diagonal, image0, own1 = pl.pallas_call(
+    store, entries, count, diagonal, image0, own0, own1 = pl.pallas_call(
         build,
         out_shape=(
             pltpu.VMEM((slots, 2, lanes, lanes), BF),
             jax.ShapeDtypeStruct((slots + 32,), jnp.int32),
             jax.ShapeDtypeStruct((1,), jnp.int32),
-            jax.ShapeDtypeStruct((owned, 4, lanes), F32),
-            jax.ShapeDtypeStruct((owned, 4, lanes), F32),
-            jax.ShapeDtypeStruct((owned, 4, lanes), F32),
+            pltpu.VMEM((owned, 4, lanes), F32),
+            pltpu.VMEM((owned, 4, lanes), F32),
+            pltpu.VMEM((owned, 4, lanes), F32),
+            pltpu.VMEM((owned, 4, lanes), F32),
         ),
-        in_specs=[SMEM_SPEC] + [VMEM_SPEC] * 7,
-        input_output_aliases={7: 0},
-        out_specs=(VMEM_SPEC, SMEM_SPEC, SMEM_SPEC, VMEM_SPEC, VMEM_SPEC, VMEM_SPEC),
+        in_specs=[SMEM_SPEC] + [VMEM_SPEC] * 6,
+        input_output_aliases={6: 0},
+        out_specs=(VMEM_SPEC, SMEM_SPEC, SMEM_SPEC) + (VMEM_SPEC,) * 4,
         scratch_shapes=[
             pltpu.VMEM((tiles, lanes, lanes), BF),
             pltpu.VMEM((owned, 48, 2 * lanes), BF),
@@ -504,7 +505,6 @@
         pair_bits,
         kept(param_ext.reshape(tiles, 8, lanes)),
         kept(field_ext.reshape(tiles, 1, lanes)),
-        own0,
         hard,
         soft,
         link,
@@ -514,33 +514,33 @@
     def halo(own, number):
         return pl.pallas_call(
             next_halo,
-            out_shape=jax.ShapeDtypeStruct(ext + (4, lanes), F32),
+            out_shape=pltpu.VMEM(ext + (4, lanes), F32),
             in_specs=[VMEM_SPEC],
             out_specs=VMEM_SPEC,
             scratch_shapes=[pltpu.SemaphoreType.DMA((1, 26)), pltpu.SemaphoreType.DMA((1, 26))],
             compiler_params=limits(2 << 20, collective_id=number, has_side_effects=True),
             name="halo",
-        )(own.reshape(nx, ny, nz, 4, lanes))
+        )(kept(own.reshape(nx, ny, nz, 4, lanes)))
 
     def operate(own, store, number):
         field = halo(own, number)
         return pl.pallas_call(
             again,
             out_shape=(
-                jax.ShapeDtypeStruct((owned, 4, lanes), F32),
-                jax.ShapeDtypeStruct((owned, 4, lanes), F32),
+                pltpu.VMEM((owned, 4, lanes), F32),
+                pltpu.VMEM((owned, 4, lanes), F32),
                 pltpu.VMEM(store.shape, BF),
             ),
-            in_specs=[VMEM_SPEC] * 4 + [SMEM_SPEC] * 2 + [VMEM_SPEC],
+            in_specs=[VMEM_SPEC] * 4 + [SMEM_SPEC] * 2 + [VMEM_SPEC] * 3,
             out_specs=(VMEM_SPEC,) * 3,
             input_output_aliases={3: 2},
             scratch_shapes=[
                 pltpu.VMEM((tiles, 16, lanes), BF),
                 pltpu.VMEM((owned + 1, 8, 2 * lanes), F32),
             ],
-            compiler_params=limits(4 << 20),
+            compiler_params=limits(8 << 20),
             name="apply",
-        )(field.reshape(tiles, 4, lanes), own, link, kept(store), entries, count, diagonal)
+        )(kept(field.reshape(tiles, 4, lanes)), kept(own), link, kept(store), entries, count, kept(diagonal), kept(param_ext), kept(field_ext))
 
     image1, own2, store = operate(own1, store, 1)
     image2, _, _ = operate(own2, store, 2)
@@ -561,7 +561,7 @@
         ],
         compiler_params=limits(4 << 20, collective_id=3, has_side_effects=True),
         name="combine",
-    )(*(own0, own1, own2, image0, image1, image2))
+    )(*(kept(a) for a in (own0, own1, own2, image0, image1, image2)))
     out = (4, nx, ny, nz, lanes)
     return answer.reshape(out), left.reshape(out)
 

time: 99.5 us -> 91.8 us (0.923)
  local copies, waits for them, and re-layouts: 8.91 us -> 1.26 us
    unnamed x32 -> x2, local copies, waits for them, and re-layouts: 8.91 us -> 1.26 us
where the time goes in v3:
time: 91.8 us
  Pallas kernels  89.8 us (98%)
  local copies, waits for them, and re-layouts  1.26 us (1%)
    pallas_call x2, Pallas kernels, halo(): pl.pallas_call(next_halo, out_shape=pltpu.VMEM(ext + (4, lanes), F32), in...  24.4 us
    pallas_call x1, Pallas kernels, on_device(): pl.pallas_call(build, out_shape=(pltpu.VMEM((slots, 2, lanes, lanes), BF)...  21.3 us
    pallas_call x1, Pallas kernels, on_device(): pl.pallas_call(combine, out_shape=(shape, shape), in_specs=[VMEM_SPEC] *...  19 us
    pallas_call x2, Pallas kernels, operate(): pl.pallas_call(again, out_shape=(pltpu.VMEM((owned, 4, lanes), F32), pltp...  14.2 us
    pallas_call x1, Pallas kernels, on_device(): pl.pallas_call(first_halo, out_shape=(pltpu.VMEM(ext + (8, lanes), F32),...  11 us

profile of v3, /device:TPU:1, one launch (start us, length us, event | category | flops | bytes accessed | tf_op | source)
XLA Modules:
  0.0 91.8 jit_solution(3224251223813199775)
XLA Ops:
  0.6 11.0 %first_halo.1 = (f32[4,4,10,8,128]{4,3,2,1,0:T(8,128)S(1)}, f32[4,4,10,1,128]{4,3,2,1,0:T(1,128)S(1)}) custom-call(f32[3,2,2,8,128]{4,3,2,1,0:T(8,128)} %pos_in.1, f32[2,2,8,128]{3,2,1,0:T(8,128)} %shield_in.1, f32[2,2,8,128]{3,2,1,0:T(8,128)} %width_in.1, f32[4,2,2,8,128]{4,3,2,1,0:T(8,128)} %rhs_in.1), custom_call_target="tpu_custom_call" | custom-call | tf_op jit(solution)/shard_map/first_halo/pallas_call | solution.py:450
  11.6 21.3 %build.1 = (bf16[864,2,128,128]{3,2,1,0:T(8,128)(2,1)S(1)}, s32[896]{0:T(1024)}, s32[1]{0:T(128)}, f32[32,4,128]{2,1,0:T(4,128)S(1)}, f32[32,4,128]{2,1,0:T(4,12...) custom-call(s32[2,2,8]{2,1,0:T(2,128)} %bits.1, ...), custom_call_target="tpu_custom_call", output_to_operand_aliasing={{0}: (6, {})} | custom-call | tf_op jit(solution)/shard_map/build/pallas_call | solution.py:482
  32.9 16.2 %halo.2 = f32[4,4,10,4,128]{4,3,2,1,0:T(4,128)S(1)} custom-call(f32[2,2,8,4,128]{4,3,2,1,0:T(4,128)S(1)} %bitcast.15), custom_call_target="tpu_custom_call" | custom-call | tf_op jit(solution)/shard_map/halo/pallas_call | solution.py:515
  49.1 6.8 %apply.2 = (f32[32,4,128]{2,1,0:T(4,128)S(1)}, f32[32,4,128]{2,1,0:T(4,128)S(1)}, bf16[864,2,128,128]{3,2,1,0:T(8,128)(2,1)S(1)}) custom-call(f32[160,4,128]{2,1,0:T(4,128)S(1)} %bitcast.13, f32[32,4,128]{2,1,0:T(4,128)S(1)} %get-tuple-element.20.own.u1, f32[4,8,128]{2,1,0:T(8,128)} %bitcast.20, ...), custom_call_target="tpu_custom_call", output_to_operand_aliasing={{2}: (3, {})} | custom-call | tf_op jit(solution)/shard_map/apply/pallas_call | solution.py:527
  55.9 8.2 %halo.3 = f32[4,4,10,4,128]{4,3,2,1,0:T(4,128)S(1)} custom-call(f32[2,2,8,4,128]{4,3,2,1,0:T(4,128)S(1)} %bitcast.16), custom_call_target="tpu_custom_call" | custom-call | tf_op jit(solution)/shard_map/halo/pallas_call | solution.py:515
  64.1 7.4 %apply.3 = (f32[32,4,128]{2,1,0:T(4,128)S(1)}, f32[32,4,128]{2,1,0:T(4,128)}, bf16[864,2,128,128]{3,2,1,0:T(8,128)(2,1)S(1)}) custom-call(f32[160,4,128]{2,1,0:T(4,128)S(1)} %bitcast.12, f32[32,4,128]{2,1,0:T(4,128)S(1)} %get-tuple-element.25.own.u2, f32[4,8,128]{2,1,0:T(8,128)} %bitcast.21, ...), custom_call_target="tpu_custom_call", output_to_operand_aliasing={{2}: (3, {})} | custom-call | tf_op jit(solution)/shard_map/apply/pallas_call | solution.py:527
  71.5 19.0 %combine.1 = (f32[4,4,8,128]{3,2,1,0:T(8,128)S(1)}, f32[4,4,8,128]{3,2,1,0:T(8,128)S(1)}) custom-call(f32[32,4,128]{2,1,0:T(4,128)S(1)} %get-tuple-element.19.u0, f32[32,4,128]{2,1,0:T(4,128)S(1)} %get-tuple-element.20.own.u1, f32[32,4,128]{2,1,0:T(4,128)S(1)} %get-tuple-element.25.own.u2, f32[32,4,128]{2,1,0:T(4,128)S(1)} %get-tuple-element.26.w0, ...), custom_call_target="tpu_custom_call" | custom-call | tf_op jit(solution)/shard_map/combine/pallas_call | solution.py:550
  90.5 0.6 copy.18
  91.1 0.6 copy.19
  (1 shorter events, 0.0 us)

commit v4 on v3

--- a/solution.py
+++ b/solution.py
@@ -16,7 +16,7 @@
 COULOMB_GAIN = 250000.0
 RESPONSE_SCALE = 0.003
 GROUP = 32
-WIDE = 32
+LIMIT = 8 << 20
 DIRECTIONS = [d for d in itertools.product((-1, 0, 1), repeat=3) if d != (0, 0, 0)]
 VMEM_SPEC = pl.BlockSpec(memory_space=pltpu.VMEM)
 SMEM_SPEC = pl.BlockSpec(memory_space=pltpu.SMEM)
@@ -56,49 +56,50 @@
     return barrier, count
 
 
-def exchange(pairs, send_sem, recv_sem):
-    def copies(index, direction, place):
-        made = []
-        for number, (own, ext) in enumerate(pairs):
-            size = own.shape[:3]
-            source = own.at[tuple(own_range(s, n) for s, n in zip(direction, size))]
-            target = ext.at[tuple(ghost_range(s, n) for s, n in zip(direction, size))]
-            made.append(
-                pltpu.make_async_remote_copy(
-                    source,
-                    target,
-                    send_sem.at[number, index],
-                    recv_sem.at[number, index],
-                    device_id=place,
-                    device_id_type=MESH,
-                )
+def rim_copies(pairs, index, direction, place, send_sem, recv_sem):
+    made = []
+    for number, (own, ext) in enumerate(pairs):
+        size = own.shape[:3]
+        made.append(
+            pltpu.make_async_remote_copy(
+                own.at[tuple(own_range(s, n) for s, n in zip(direction, size))],
+                ext.at[tuple(ghost_range(s, n) for s, n in zip(direction, size))],
+                send_sem.at[number, index],
+                recv_sem.at[number, index],
+                device_id=place,
+                device_id_type=MESH,
             )
-        return made
-
+        )
+    return made
+
+
+def send_rims(pairs, send_sem, recv_sem):
     for index, direction in enumerate(DIRECTIONS):
         place, exists = neighbour(direction)
 
         @pl.when(exists)
         def _():
-            for copy in copies(index, direction, place):
+            for copy in rim_copies(pairs, index, direction, place, send_sem, recv_sem):
                 copy.start()
 
+
+def await_rims(pairs, send_sem, recv_sem):
     for index, direction in enumerate(DIRECTIONS):
         place, exists = neighbour(direction)
         source, incoming = neighbour(tuple(-s for s in direction))
 
         @pl.when(incoming)
         def _():
-            for copy in copies(index, direction, place):
+            for copy in rim_copies(pairs, index, direction, place, send_sem, recv_sem):
                 copy.wait_recv()
 
         @pl.when(exists)
         def _():
-            for copy in copies(index, direction, place):
+            for copy in rim_copies(pairs, index, direction, place, send_sem, recv_sem):
                 copy.wait_send()
 
 
-def first_halo(pos_in, shield_in, width_in, rhs_in, param_ext, field_ext, *scratch):
+def first_halo(pos_in, shield_in, width_in, rhs_in, param_ext, field_ext, store, *scratch):
     param_own, last_own, pos, shield, width, rhs, load_sem, send_sem, recv_sem = scratch
     loads = [
         pltpu.make_async_copy(source, target, load_sem.at[index])
@@ -128,15 +129,16 @@
                         last_own[x, y, z] = row
                         field_ext[x + 1, y + 1, z + 1] = row
     pl.semaphore_wait(barrier, count)
-    exchange(((param_own, param_ext), (last_own, field_ext)), send_sem, recv_sem)
-
-
-def next_halo(own, ext, send_sem, recv_sem):
-    ext[...] = jnp.zeros_like(ext)
-    barrier, count = greet()
-    ext[1:-1, 1:-1, 1:-1] = own[...]
-    pl.semaphore_wait(barrier, count)
-    exchange(((own, ext),), send_sem, recv_sem)
+    pairs = ((param_own, param_ext), (last_own, field_ext))
+    send_rims(pairs, send_sem, recv_sem)
+    slots = store.shape[0]
+
+    def clear(index, carry):
+        store[pl.ds(index * 5, 5)] = jnp.zeros((5,) + store.shape[1:], BF)
+        return carry
+
+    lax.fori_loop(0, slots // 5, clear, 0)
+    await_rims(pairs, send_sem, recv_sem)
 
 
 def split3(value):
@@ -200,15 +202,14 @@
     lax.fori_loop(0, tiles // 16, step, 0)
 
 
-def apply_group(base, size, entries, halves, window, acc):
-    rows = acc.shape[1]
+def apply_group(base, size, entries, halves, store, acc):
     for sub in range(size):
         code = entries[base + sub]
         e = code & 255
-        t = lax.shift_right_logical(code, 16)
-        both = jnp.concatenate([window[sub, 0], window[sub, 1]], axis=1)
-        out = jnp.dot(halves[e], both, preferred_element_type=F32)
-        acc[t] = acc[t] + out[:rows]
+        t = lax.shift_right_logical(code, 14) & 63
+        slot = lax.shift_right_logical(code, 20)
+        both = jnp.concatenate([store[slot, 0], store[slot, 1]], axis=1)
+        acc[t] = acc[t] + jnp.dot(halves[e], both, preferred_element_type=F32)
 
 
 def image_rows(out, diagonal, link, value):
@@ -231,8 +232,8 @@
 
 
 def build(
-    bits, param, field, hardness, softness, coupling, blank, store, entries, count, diagonal, image, own, send,
-    features, mine, halves, acc
+    bits, param, field, hardness, softness, coupling, blank, store, diagonal, image, own, send,
+    features, mine, halves, acc, entries
 ):
     ey_size, ez_size = 4, 10
     half = (2.0, 2.0, 5.0)
@@ -255,21 +256,20 @@
             y = lax.shift_right_logical(t, 3) & 1
             z = t & 7
             word = bits[x, y, z]
-            own_code = ((x + 1) * ey_size + y + 1) * ez_size + z + 1 + 65792 * t
-            entries[t] = own_code
+            own_code = ((x + 1) * ey_size + y + 1) * ez_size + z + 1 + 256 * t + 16384 * t + (27 << 20) * t
+            entries[t] = own_code + (13 << 20)
             for code in range(27):
                 if code == 13:
                     continue
                 shift = ((code // 9 - 1) * ey_size + (code // 3 % 3 - 1)) * ez_size + code % 3 - 1
-                entries[at] = own_code + shift
+                entries[at] = own_code + shift + (code << 20)
                 at = at + (lax.shift_right_logical(word, code) & 1)
         return at
 
     total = lax.fori_loop(0, 16, features_step, jnp.int32(owned))
     middle = (ey_size + 1) * ez_size + 1
-    for sub in range(WIDE):
-        entries[total + sub] = middle + 65536 * owned
-    count[0] = total
+    for sub in range(GROUP):
+        entries[total + sub] = middle + 16384 * owned + ((27 * owned) << 20)
 
     def own_step(index, carry):
         ex = lax.shift_right_logical(index, 1) + 1
@@ -284,10 +284,11 @@
     split_fields(lambda e: jnp.concatenate([param[e, 5:8, :], field[e]], axis=0), halves, tiles)
     acc[...] = jnp.zeros_like(acc)
 
-    def pair(slot, window, sub, masked):
-        code = entries[slot]
+    def pair(position, masked):
+        code = entries[position]
         e = code & 255
-        t = lax.shift_right_logical(code, 8) & 255
+        t = lax.shift_right_logical(code, 8) & 63
+        slot = lax.shift_right_logical(code, 20)
         both = jnp.dot(features[e, :, 0:48], mine[t], preferred_element_type=F32)
         partner_width = jnp.broadcast_to(param[e, 4:5, :], (128, 128)).T
         widths = partner_width + param[place_of(t), 4:5, :]
@@ -299,13 +300,12 @@
             )
             coulomb = jnp.where(same, 0.0, coulomb)
             response = jnp.where(same, 0.0, response)
-        window[sub, 0] = coulomb.astype(BF)
-        window[sub, 1] = response.astype(BF)
+        store[slot, 0] = coulomb.astype(BF)
+        store[slot, 1] = response.astype(BF)
 
     def self_step(index, carry):
-        window = store.at[pl.ds(index * 8, 8)]
         for sub in range(8):
-            pair(index * 8 + sub, window, sub, True)
+            pair(index * 8 + sub, True)
         return carry
 
     lax.fori_loop(0, owned // 8, self_step, 0)
@@ -313,16 +313,15 @@
 
     def pair_step(index, carry):
         base = owned + index * GROUP
-        window = store.at[pl.ds(base - GROUP, 2 * GROUP)]
-        apply_group(base - GROUP, GROUP, entries, halves, window, acc)
+        apply_group(base - GROUP, GROUP, entries, halves, store, acc)
         for sub in range(GROUP):
-            pair(base + sub, window, GROUP + sub, False)
+            pair(base + sub, False)
         return carry
 
     groups = (total - owned + GROUP - 1) // GROUP
     lax.fori_loop(0, groups, pair_step, 0)
     last = owned + (groups - 1) * GROUP
-    apply_group(last, GROUP, entries, halves, store.at[pl.ds(last, GROUP)], acc)
+    apply_group(last, GROUP, entries, halves, store, acc)
     row = lax.broadcasted_iota(jnp.int32, (4, 128), 0)
 
     def make(index, sub):
@@ -338,27 +337,14 @@
     finish_all(owned, make)
 
 
-def again(field, own, coupling, store, entries, count, diagonal, unused, idle, image, send, passed, halves, acc):
-    owned = 32
-    split_fields(lambda e: field[e], halves, field.shape[0])
-    acc[...] = jnp.zeros_like(acc)
-
-    def step(index, carry):
-        apply_group(index * WIDE, WIDE, entries, halves, store.at[pl.ds(index * WIDE, WIDE)], acc)
-        return carry
-
-    lax.fori_loop(0, (count[0] + WIDE - 1) // WIDE, step, 0)
-
-    def make(index, sub):
-        value = own[index * 8 + sub]
-        diag = diagonal[index * 8 + sub]
-        made = image_rows(acc[index * 8 + sub], diag, coupling[index, sub : sub + 1, :], value)
-        return (image, send), (made, made - SHIFT * value)
-
-    finish_all(owned, make)
-
-
-def combine(u0, u1, u2, w0, w1, w2, solution, residual, part, plane, line, send_sem, recv_sem):
+INSIDE = {0: (0, 1), 1: (-1, 0)}
+FLAT = list(itertools.product((-1, 0, 1), repeat=2))
+
+
+def solve(u0, u1, w0, diagonal, coupling, store, unused, idle, solution, residual, *scratch):
+    ext1, ext2, u2, w1, w2, halves, acc, part, plane, line, rim_send, rim_recv, send_sem, recv_sem = scratch
+    nx, ny, nz = u1.shape[:3]
+    ey_size, ez_size = ny + 2, nz + 2
     sizes = [lax.axis_size(axis) for axis in AXES]
     gx, gy, gz = (lax.axis_index(axis) for axis in AXES)
     across = []
@@ -367,18 +353,134 @@
             if a or b:
                 across.append((gx, lax.rem(gy + a, sizes[1]), lax.rem(gz + b, sizes[2])))
     along = [(lax.rem(gx + a, sizes[0]), gy, gz) for a in range(1, sizes[0])]
-    barrier = pltpu.get_barrier_semaphore()
+    ext1[...] = jnp.zeros_like(ext1)
+    ext2[...] = jnp.zeros_like(ext2)
+    barrier, count = greet()
     for peer in across + along:
         pl.semaphore_signal(barrier, inc=1, device_id=peer, device_id_type=MESH)
 
-    wanted = [(u0, u0), (u0, u1), (u0, u2), (u0, w0), (u0, w1), (u0, w2), (u1, w1), (u1, w2), (u2, w2)]
+    def split_columns(ext, lowest, columns, rows, depth):
+        def step(index, carry):
+            x = index // columns + lowest
+            y = index % columns + lowest
+            values = [ext[x, y, z] for z in depth]
+            parts = []
+            for value in values:
+                high = value.astype(BF).astype(F32)
+                parts.append(jnp.concatenate([high, value - high, jnp.zeros((8, 128), F32)], axis=0).astype(BF))
+            for z, made in zip(depth, parts):
+                halves[(x * ey_size + y) * ez_size + z] = made
+            return carry
+
+        lax.fori_loop(0, columns * rows, step, 0)
+
+    def tile_sum(x, y, z, offsets):
+        total = None
+        for dx, dy, dz in offsets:
+            slot = ((x * ny + y) * nz + z) * 27 + (dx + 1) * 9 + (dy + 1) * 3 + dz + 1
+            e = ((x + 1 + dx) * ey_size + y + 1 + dy) * ez_size + z + 1 + dz
+            both = jnp.concatenate([store[slot, 0], store[slot, 1]], axis=1)
+            out = jnp.dot(halves[e], both, preferred_element_type=F32)
+            total = out if total is None else total + out
+        return total[:8]
+
+    columns = [(x, y) for x in range(nx) for y in range(ny)]
+
+    def inside(x, y):
+        return [(dx, dy) for dx in INSIDE[x] for dy in INSIDE[y]]
+
+    def outside(x, y):
+        return [d for d in FLAT if d not in inside(x, y)]
+
+    def level_pass():
+        def step(index, carry):
+            for sub in range(2):
+                z = index * 2 + sub
+                for x, y in columns:
+                    acc[(x * ny + y) * nz + z] = tile_sum(x, y, z, [d + (0,) for d in inside(x, y)])
+            return carry
+
+        lax.fori_loop(0, nz // 2, step, 0)
+
+    def between_pass():
+        def step(z, carry):
+            for x, y in columns:
+                t = (x * ny + y) * nz + z
+                acc[t] = acc[t] + tile_sum(x, y, z, [d + (1,) for d in inside(x, y)])
+                acc[t + 1] = acc[t + 1] + tile_sum(x, y, z + 1, [d + (-1,) for d in inside(x, y)])
+            return carry
+
+        lax.fori_loop(0, nz - 1, step, 0)
+
+    def rim_pass():
+        for x, y in columns:
+            for z, dz in ((0, -1), (nz - 1, 1)):
+                t = (x * ny + y) * nz + z
+                acc[t] = acc[t] + tile_sum(x, y, z, [d + (dz,) for d in inside(x, y)])
+
+        def step(index, carry):
+            for sub in range(2):
+                z = index * 2 + sub
+                for x, y in columns:
+                    t = (x * ny + y) * nz + z
+                    around = [d + (dz,) for d in outside(x, y) for dz in (-1, 0, 1)]
+                    acc[t] = acc[t] + tile_sum(x, y, z, around)
+            return carry
+
+        lax.fori_loop(0, nz // 2, step, 0)
+
+    def finish(vector, image, following):
+        def step(index, carry):
+            x = index // ny
+            y = index % ny
+            made = []
+            for z in range(nz):
+                t = index * nz + z
+                value = vector[x, y, z]
+                out = image_rows(acc[t], diagonal[t], coupling[index, z : z + 1, :], value)
+                made.append((out, out - SHIFT * value))
+            for z, (out, rest) in enumerate(made):
+                image[index * nz + z] = out
+                if following is not None:
+                    following[x, y, z] = rest
+            return carry
+
+        lax.fori_loop(0, nx * ny, step, 0)
+
+    own_depth = range(1, nz + 1)
+    whole = range(nz + 2)
+    ext1[1:-1, 1:-1, 1:-1] = u1[...]
+    split_columns(ext1, 1, ny, nx, own_depth)
+    level_pass()
+    pl.semaphore_wait(barrier, count + (len(across) + len(along)))
+    send_rims(((u1, ext1),), rim_send.at[pl.ds(0, 1)], rim_recv.at[pl.ds(0, 1)])
+    between_pass()
+    await_rims(((u1, ext1),), rim_send.at[pl.ds(0, 1)], rim_recv.at[pl.ds(0, 1)])
+    split_columns(ext1, 0, ny + 2, nx + 2, whole)
+    rim_pass()
+    finish(u1, w1, u2)
+
+    ext2[1:-1, 1:-1, 1:-1] = u2[...]
+    split_columns(ext2, 1, ny, nx, own_depth)
+    send_rims(((u2, ext2),), rim_send.at[pl.ds(1, 1)], rim_recv.at[pl.ds(1, 1)])
+    level_pass()
+    between_pass()
+    await_rims(((u2, ext2),), rim_send.at[pl.ds(1, 1)], rim_recv.at[pl.ds(1, 1)])
+    split_columns(ext2, 0, ny + 2, nx + 2, whole)
+    rim_pass()
+    finish(u2, w2, None)
+
+    owned = nx * ny * nz
+    tile = (owned, 4, 128)
+    b0, b1, b2 = (u[...].reshape(tile) for u in (u0, u1, u2))
+    a0, a1, a2 = (w[...].reshape(tile) for w in (w0, w1, w2))
+    wanted = [(b0, b0), (b0, b1), (b0, b2), (b0, a0), (b0, a1), (b0, a2), (b1, a1), (b1, a2), (b2, a2)]
     sums = []
     for left, right in wanted:
-        both = jnp.sum(left[...] * right[...], axis=0)
+        both = jnp.sum(left * right, axis=0)
         sums.append(both[0:2] + both[2:4])
     stacked = jnp.concatenate(sums + [jnp.zeros((128 - 18, 128), F32)], axis=0)
     part[0] = jnp.sum(stacked.T, axis=0, keepdims=True)
-    pl.semaphore_wait(barrier, len(across) + len(along))
 
     def gather(turn, peers, here, stage, width):
         made = []
@@ -423,8 +525,8 @@
         return jnp.concatenate(pair + pair, axis=0)[None]
 
     c0, c1, c2 = (spread(c) for c in (c0, c1, c2))
-    answer = c0 * u0[...] + c1 * u1[...] + c2 * u2[...]
-    left = u0[...] - (c0 * w0[...] + c1 * w1[...] + c2 * w2[...])
+    answer = c0 * b0 + c1 * b1 + c2 * b2
+    left = b0 - (c0 * a0 + c1 * a1 + c2 * a2)
     for t in range(32):
         for f in range(4):
             solution[f, t // 8, t % 8 : t % 8 + 1, :] = answer[t, f : f + 1]
@@ -436,7 +538,6 @@
     owned = nx * ny * nz
     ext = (nx + 2, ny + 2, nz + 2)
     tiles = ext[0] * ext[1] * ext[2]
-    slots = owned * 27
 
     def kept(value):
         return pltpu.with_memory_space_constraint(value, pltpu.VMEM)
@@ -447,14 +548,16 @@
     def limits(size, **more):
         return pltpu.CompilerParams(vmem_limit_bytes=size, **more)
 
-    param_ext, field_ext = pl.pallas_call(
+    slots = owned * 27 + 3
+    param_ext, field_ext, blank = pl.pallas_call(
         first_halo,
         out_shape=(
             pltpu.VMEM(ext + (8, lanes), F32),
             pltpu.VMEM(ext + (1, lanes), F32),
+            pltpu.VMEM((slots - slots % 5, 2, lanes, lanes), BF),
         ),
         in_specs=[pl.BlockSpec(memory_space=pltpu.HBM)] * 4,
-        out_specs=(VMEM_SPEC,) * 2,
+        out_specs=(VMEM_SPEC,) * 3,
         scratch_shapes=[
             pltpu.VMEM((nx, ny, nz, 8, lanes), F32),
             pltpu.VMEM((nx, ny, nz, 1, lanes), F32),
@@ -466,40 +569,25 @@
             pltpu.SemaphoreType.DMA((2, 26)),
             pltpu.SemaphoreType.DMA((2, 26)),
         ],
-        compiler_params=limits(4 << 20, collective_id=0, has_side_effects=True),
+        compiler_params=limits(LIMIT, collective_id=0, has_side_effects=True),
         name="first_halo",
     )(*(far(a) for a in (positions, shield, width, right_side)))
 
     hard, soft, link = (a.reshape(owned // 8, 8, lanes) for a in (hardness, softness, coupling))
-    vector = jax.ShapeDtypeStruct((owned, 4, lanes), F32)
-    blank = pl.pallas_call(
-        lambda ref: None,
-        out_shape=pltpu.VMEM((slots, 2, lanes, lanes), BF),
-        out_specs=VMEM_SPEC,
-        compiler_params=limits(8 << 20),
-        name="reserve",
-    )()
-    store, entries, count, diagonal, image0, own0, own1 = pl.pallas_call(
+    store, diagonal, image0, own0, own1 = pl.pallas_call(
         build,
-        out_shape=(
-            pltpu.VMEM((slots, 2, lanes, lanes), BF),
-            jax.ShapeDtypeStruct((slots + 32,), jnp.int32),
-            jax.ShapeDtypeStruct((1,), jnp.int32),
-            pltpu.VMEM((owned, 4, lanes), F32),
-            pltpu.VMEM((owned, 4, lanes), F32),
-            pltpu.VMEM((owned, 4, lanes), F32),
-            pltpu.VMEM((owned, 4, lanes), F32),
-        ),
+        out_shape=(pltpu.VMEM(blank.shape, BF),) + (pltpu.VMEM((owned, 4, lanes), F32),) * 4,
         in_specs=[SMEM_SPEC] + [VMEM_SPEC] * 6,
         input_output_aliases={6: 0},
-        out_specs=(VMEM_SPEC, SMEM_SPEC, SMEM_SPEC) + (VMEM_SPEC,) * 4,
+        out_specs=(VMEM_SPEC,) * 5,
         scratch_shapes=[
             pltpu.VMEM((tiles, lanes, lanes), BF),
             pltpu.VMEM((owned, 48, 2 * lanes), BF),
             pltpu.VMEM((tiles, 16, lanes), BF),
             pltpu.VMEM((owned + 1, 16, 2 * lanes), F32),
+            pltpu.SMEM((owned * 27 + GROUP,), jnp.int32),
         ],
-        compiler_params=limits(8 << 20),
+        compiler_params=limits(LIMIT),
         name="build",
     )(
         pair_bits,
@@ -511,57 +599,34 @@
         kept(blank),
     )
 
-    def halo(own, number):
-        return pl.pallas_call(
-            next_halo,
-            out_shape=pltpu.VMEM(ext + (4, lanes), F32),
-            in_specs=[VMEM_SPEC],
-            out_specs=VMEM_SPEC,
-            scratch_shapes=[pltpu.SemaphoreType.DMA((1, 26)), pltpu.SemaphoreType.DMA((1, 26))],
-            compiler_params=limits(2 << 20, collective_id=number, has_side_effects=True),
-            name="halo",
-        )(kept(own.reshape(nx, ny, nz, 4, lanes)))
-
-    def operate(own, store, number):
-        field = halo(own, number)
-        return pl.pallas_call(
-            again,
-            out_shape=(
-                pltpu.VMEM((owned, 4, lanes), F32),
-                pltpu.VMEM((owned, 4, lanes), F32),
-                pltpu.VMEM(store.shape, BF),
-            ),
-            in_specs=[VMEM_SPEC] * 4 + [SMEM_SPEC] * 2 + [VMEM_SPEC] * 3,
-            out_specs=(VMEM_SPEC,) * 3,
-            input_output_aliases={3: 2},
-            scratch_shapes=[
-                pltpu.VMEM((tiles, 16, lanes), BF),
-                pltpu.VMEM((owned + 1, 8, 2 * lanes), F32),
-            ],
-            compiler_params=limits(8 << 20),
-            name="apply",
-        )(kept(field.reshape(tiles, 4, lanes)), kept(own), link, kept(store), entries, count, kept(diagonal), kept(param_ext), kept(field_ext))
-
-    image1, own2, store = operate(own1, store, 1)
-    image2, _, _ = operate(own2, store, 2)
     line = lax.axis_size("gx")
     plane = lax.axis_size("gy") * lax.axis_size("gz")
     shape = jax.ShapeDtypeStruct((4, owned // 8, 8, lanes), F32)
     answer, left = pl.pallas_call(
-        combine,
+        solve,
         out_shape=(shape, shape),
-        in_specs=[VMEM_SPEC] * 6,
+        in_specs=[VMEM_SPEC] * 8,
         out_specs=(VMEM_SPEC, VMEM_SPEC),
         scratch_shapes=[
+            pltpu.VMEM(ext + (4, lanes), F32),
+            pltpu.VMEM(ext + (4, lanes), F32),
+            pltpu.VMEM((nx, ny, nz, 4, lanes), F32),
+            pltpu.VMEM((owned, 4, lanes), F32),
+            pltpu.VMEM((owned, 4, lanes), F32),
+            pltpu.VMEM((tiles, 16, lanes), BF),
+            pltpu.VMEM((owned, 8, 2 * lanes), F32),
             pltpu.VMEM((2, 1, lanes), F32),
             pltpu.VMEM((plane, 1, lanes), F32),
             pltpu.VMEM((line, 1, lanes), F32),
+            pltpu.SemaphoreType.DMA((2, 26)),
+            pltpu.SemaphoreType.DMA((2, 26)),
             pltpu.SemaphoreType.DMA((2, plane - 1)),
             pltpu.SemaphoreType.DMA((2, plane - 1)),
         ],
-        compiler_params=limits(4 << 20, collective_id=3, has_side_effects=True),
-        name="combine",
-    )(*(kept(a) for a in (own0, own1, own2, image0, image1, image2)))
+        compiler_params=limits(LIMIT, collective_id=1, has_side_effects=True),
+        name="solve",
+    )(kept(own0), kept(own1.reshape(nx, ny, nz, 4, lanes)), kept(image0), kept(diagonal), link, kept(store),
+      kept(param_ext.reshape(tiles, 8, lanes)), kept(field_ext.reshape(tiles, 1, lanes)))
     out = (4, nx, ny, nz, lanes)
     return answer.reshape(out), left.reshape(out)
 

time: 91.8 us -> 85.4 us (0.930)
  Pallas kernels: 89.8 us -> 80.9 us
  local copies, waits for them, and re-layouts: 1.26 us -> 2.95 us
    pallas_call x7 -> x2, Pallas kernels: 78.8 us -> 66.7 us  [the longest x1 45.8 us: on_device(): pl.pallas_call(solve, out_shape=(shape, shape), in_specs=[VMEM_SPEC] * 8,...]
    pallas_call x1, Pallas kernels: 11 us -> 14.2 us  [on_device(): pl.pallas_call(first_halo, out_shape=(pltpu.VMEM(ext + (8, lanes), F32),...]
    unnamed x2, local copies, waits for them, and re-layouts: 1.26 us -> 2.95 us
where the time goes in v4:
time: 85.4 us; the launch traced here: 84.5 us
  Pallas kernels  80.9 us (95%)
  local copies, waits for them, and re-layouts  2.95 us (3%)
    pallas_call x1, Pallas kernels, on_device(): pl.pallas_call(solve, out_shape=(shape, shape), in_specs=[VMEM_SPEC] * 8,...  45.8 us
    pallas_call x1, Pallas kernels, on_device(): pl.pallas_call(build, out_shape=(pltpu.VMEM(blank.shape, BF),) + (pltpu.V...  20.8 us
    pallas_call x1, Pallas kernels, on_device(): pl.pallas_call(first_halo, out_shape=(pltpu.VMEM(ext + (8, lanes), F32),...  14.2 us
    unnamed x2, local copies, waits for them, and re-layouts  2.95 us

profile of v4, /device:TPU:1, one launch (start us, length us, event | category | flops | bytes accessed | tf_op | source)
XLA Modules:
  0.0 84.5 jit_solution(3546893962564097521)
XLA Ops:
  0.6 14.2 %first_halo.1 = (f32[4,4,10,8,128]{4,3,2,1,0:T(8,128)S(1)}, f32[4,4,10,1,128]{4,3,2,1,0:T(1,128)S(1)}, bf16[865,2,128,128]{3,2,1,0:T(8,128)(2,1)S(1)}) custom-call(f32[3,2,2,8,128]{4,3,2,1,0:T(8,128)} %pos_in.1, f32[2,2,8,128]{3,2,1,0:T(8,128)} %shield_in.1, f32[2,2,8,128]{3,2,1,0:T(8,128)} %width_in.1, f32[4,2,2,8,128]{4,3,2,1,0:T(8,128)} %rhs_in.1), custom_call_target="tpu_custom_call" | custom-call | tf_op jit(solution)/shard_map/first_halo/pallas_call | solution.py:552
  14.8 20.8 %build.1 = (bf16[865,2,128,128]{3,2,1,0:T(8,128)(2,1)S(1)}, f32[32,4,128]{2,1,0:T(4,128)S(1)}, f32[32,4,128]{2,1,0:T(4,128)S(1)}, f32[32,4,128]{2,1,0:T(4,128)S(1)}, f32[32,4,128]{2,1,0:T(4,128)S(1)}) custom-call(s32[2,2,8]{2,1,0:T(2,128)} %bits.1, f32[160,8,128]{2,1,0:T(8,128)S(1)} %bitcast.8, ...), custom_call_target="tpu_custom_call", output_to_operand_aliasing={{0}: (6, {})} | custom-call | tf_op jit(solution)/shard_map/build/pallas_call | solution.py:577
  35.7 45.8 %solve.1 = (f32[4,4,8,128]{3,2,1,0:T(8,128)}, f32[4,4,8,128]{3,2,1,0:T(8,128)}) custom-call(f32[32,4,128]{2,1,0:T(4,128)S(1)} %get-tuple-element.15.u0, f32[2,2,8,4,128]{4,3,2,1,0:T(4,128)S(1)} %bitcast.12, f32[32,4,128]{2,1,0:T(4,128)S(1)} %get-tuple-element.17.w0, f32[32,4,128]{2,1,0:T(4,128)S(1)} %get-tuple-element.18.diagonal, f32[4,8,128]{2,1,0:T(8,128)} %bitcast.14, ...), custom_call_target="tpu_custom_call" | custom-call | tf_op jit(solution)/shard_map/solve/pallas_call | solution.py:605
  81.5 1.5 %copy.14 = f32[4,2,2,8,128]{4,3,2,1,0:T(8,128)} copy(f32[4,2,2,8,128]{4,3,2,1,0:T(8,128)} %bitcast.16) | data formatting | bytes 131072
  83.0 1.5 %copy.15 = f32[4,2,2,8,128]{4,3,2,1,0:T(8,128)} copy(f32[4,2,2,8,128]{4,3,2,1,0:T(8,128)} %bitcast.15) | data formatting | bytes 131072

commit v5 on v4

--- a/solution.py
+++ b/solution.py
@@ -15,8 +15,8 @@
 LOG2E = 1.4426950408889634
 COULOMB_GAIN = 250000.0
 RESPONSE_SCALE = 0.003
-GROUP = 32
-LIMIT = 8 << 20
+GROUP = 16
+LIMIT = 8800000
 DIRECTIONS = [d for d in itertools.product((-1, 0, 1), repeat=3) if d != (0, 0, 0)]
 VMEM_SPEC = pl.BlockSpec(memory_space=pltpu.VMEM)
 SMEM_SPEC = pl.BlockSpec(memory_space=pltpu.SMEM)
@@ -202,12 +202,12 @@
     lax.fori_loop(0, tiles // 16, step, 0)
 
 
-def apply_group(base, size, entries, halves, store, acc):
+def apply_group(base, size, entries, halves, store, acc, recent=False):
     for sub in range(size):
         code = entries[base + sub]
         e = code & 255
         t = lax.shift_right_logical(code, 14) & 63
-        slot = lax.shift_right_logical(code, 20)
+        slot = sub if recent else lax.shift_right_logical(code, 20)
         both = jnp.concatenate([store[slot, 0], store[slot, 1]], axis=1)
         acc[t] = acc[t] + jnp.dot(halves[e], both, preferred_element_type=F32)
 
@@ -233,7 +233,7 @@
 
 def build(
     bits, param, field, hardness, softness, coupling, blank, store, diagonal, image, own, send,
-    features, mine, halves, acc, entries
+    features, mine, halves, acc, entries, recent
 ):
     ey_size, ez_size = 4, 10
     half = (2.0, 2.0, 5.0)
@@ -284,7 +284,7 @@
     split_fields(lambda e: jnp.concatenate([param[e, 5:8, :], field[e]], axis=0), halves, tiles)
     acc[...] = jnp.zeros_like(acc)
 
-    def pair(position, masked):
+    def pair(position, sub, masked):
         code = entries[position]
         e = code & 255
         t = lax.shift_right_logical(code, 8) & 63
@@ -298,30 +298,31 @@
             same = lax.broadcasted_iota(jnp.int32, (128, 128), 0) == lax.broadcasted_iota(
                 jnp.int32, (128, 128), 1
             )
-            coulomb = jnp.where(same, 0.0, coulomb)
-            response = jnp.where(same, 0.0, response)
-        store[slot, 0] = coulomb.astype(BF)
-        store[slot, 1] = response.astype(BF)
+            coulomb = jnp.where(same, 0.0, coulomb.astype(F32))
+            response = jnp.where(same, 0.0, response.astype(F32))
+        for side, value in enumerate((coulomb.astype(BF), response.astype(BF))):
+            recent[sub, side] = value
+            store[slot, side] = value
 
     def self_step(index, carry):
-        for sub in range(8):
-            pair(index * 8 + sub, True)
+        for sub in range(GROUP):
+            pair(index * GROUP + sub, sub, True)
         return carry
 
-    lax.fori_loop(0, owned // 8, self_step, 0)
+    lax.fori_loop(0, owned // GROUP, self_step, 0)
     apply_group(0, owned - GROUP, entries, halves, store, acc)
 
     def pair_step(index, carry):
         base = owned + index * GROUP
-        apply_group(base - GROUP, GROUP, entries, halves, store, acc)
         for sub in range(GROUP):
-            pair(base + sub, False)
+            apply_group(base - GROUP + sub, 1, entries, halves, recent.at[pl.ds(sub, 1)], acc, True)
+            pair(base + sub, sub, False)
         return carry
 
     groups = (total - owned + GROUP - 1) // GROUP
     lax.fori_loop(0, groups, pair_step, 0)
     last = owned + (groups - 1) * GROUP
-    apply_group(last, GROUP, entries, halves, store, acc)
+    apply_group(last, GROUP, entries, halves, recent, acc, True)
     row = lax.broadcasted_iota(jnp.int32, (4, 128), 0)
 
     def make(index, sub):
@@ -586,6 +587,7 @@
             pltpu.VMEM((tiles, 16, lanes), BF),
             pltpu.VMEM((owned + 1, 16, 2 * lanes), F32),
             pltpu.SMEM((owned * 27 + GROUP,), jnp.int32),
+            pltpu.VMEM((GROUP, 2, lanes, lanes), BF),
         ],
         compiler_params=limits(LIMIT),
         name="build",
@@ -601,7 +603,7 @@
 
     line = lax.axis_size("gx")
     plane = lax.axis_size("gy") * lax.axis_size("gz")
-    shape = jax.ShapeDtypeStruct((4, owned // 8, 8, lanes), F32)
+    shape = pltpu.VMEM((4, owned // 8, 8, lanes), F32)
     answer, left = pl.pallas_call(
         solve,
         out_shape=(shape, shape),

time: 85.4 us -> 81.6 us (0.956)
  Pallas kernels: 80.9 us -> 79.2 us
  local copies, waits for them, and re-layouts: 2.95 us -> 1.26 us
    unnamed x2, local copies, waits for them, and re-layouts: 2.95 us -> 1.26 us
    pallas_call x1, Pallas kernels: 45.8 us -> 44.9 us  [on_device(): pl.pallas_call(solve, out_shape=(shape, shape), in_specs=[VMEM_SPEC] * 8,...]
where the time goes in v5:
time: 81.6 us; the launch traced here: 81.1 us
  Pallas kernels  79.2 us (97%)
  local copies, waits for them, and re-layouts  1.26 us (2%)
    pallas_call x1, Pallas kernels, on_device(): pl.pallas_call(solve, out_shape=(shape, shape), in_specs=[VMEM_SPEC] * 8,...  44.9 us
    pallas_call x1, Pallas kernels, on_device(): pl.pallas_call(build, out_shape=(pltpu.VMEM(blank.shape, BF),) + (pltpu.V...  20.1 us
    pallas_call x1, Pallas kernels, on_device(): pl.pallas_call(first_halo, out_shape=(pltpu.VMEM(ext + (8, lanes), F32),...  14.2 us

profile of v5, /device:TPU:1, one launch (start us, length us, event | category | flops | bytes accessed | tf_op | source)
XLA Modules:
  0.0 81.1 jit_solution(6614286718881825163)
XLA Ops:
  0.6 14.2 %first_halo.1 = (f32[4,4,10,8,128]{4,3,2,1,0:T(8,128)S(1)}, f32[4,4,10,1,128]{4,3,2,1,0:T(1,128)S(1)}, bf16[865,2,128,128]{3,2,1,0:T(8,128)(2,1)S(1)}) custom-call(f32[3,2,2,8,128]{4,3,2,1,0:T(8,128)} %pos_in.1, f32[2,2,8,128]{3,2,1,0:T(8,128)} %shield_in.1, f32[2,2,8,128]{3,2,1,0:T(8,128)} %width_in.1, f32[4,2,2,8,128]{4,3,2,1,0:T(8,128)} %rhs_in.1), custom_call_target="tpu_custom_call" | custom-call | tf_op jit(solution)/shard_map/first_halo/pallas_call | solution.py:553
  14.8 20.1 %build.1 = (bf16[865,2,128,128]{3,2,1,0:T(8,128)(2,1)S(1)}, f32[32,4,128]{2,1,0:T(4,128)S(1)}, f32[32,4,128]{2,1,0:T(4,128)S(1)}, f32[32,4,128]{2,1,0:T(4,128)S(1)}, f32[32,4,128]{2,1,0:T(4,128)S(1)}) custom-call(s32[2,2,8]{2,1,0:T(2,128)} %bits.1, f32[160,8,128]{2,1,0:T(8,128)S(1)} %bitcast.10, ...), custom_call_target="tpu_custom_call", output_to_operand_aliasing={{0}: (6, {})} | custom-call | tf_op jit(solution)/shard_map/build/pallas_call | solution.py:578
  34.9 44.9 %solve.1 = (f32[4,4,8,128]{3,2,1,0:T(8,128)S(1)}, f32[4,4,8,128]{3,2,1,0:T(8,128)S(1)}) custom-call(f32[32,4,128]{2,1,0:T(4,128)S(1)} %get-tuple-element.15.u0, f32[2,2,8,4,128]{4,3,2,1,0:T(4,128)S(1)} %bitcast.14, f32[32,4,128]{2,1,0:T(4,128)S(1)} %get-tuple-element.17.w0, f32[32,4,128]{2,1,0:T(4,128)S(1)} %get-tuple-element.18.diagonal, ...), custom_call_target="tpu_custom_call" | custom-call | tf_op jit(solution)/shard_map/solve/pallas_call | solution.py:607
  79.8 0.6 copy.14
  80.5 0.6 copy.15

commit v6 on v5

--- a/solution.py
+++ b/solution.py
@@ -100,7 +100,7 @@
 
 
 def first_halo(pos_in, shield_in, width_in, rhs_in, param_ext, field_ext, store, *scratch):
-    param_own, last_own, pos, shield, width, rhs, load_sem, send_sem, recv_sem = scratch
+    param_own, last_own, empty, pos, shield, width, rhs, load_sem, send_sem, recv_sem = scratch
     loads = [
         pltpu.make_async_copy(source, target, load_sem.at[index])
         for index, (source, target) in enumerate(
@@ -111,6 +111,7 @@
         load.start()
     param_ext[...] = jnp.zeros_like(param_ext)
     field_ext[...] = jnp.zeros_like(field_ext)
+    empty[...] = jnp.zeros_like(empty)
     barrier, count = greet()
     for load in loads:
         load.wait()
@@ -134,7 +135,10 @@
     slots = store.shape[0]
 
     def clear(index, carry):
-        store[pl.ds(index * 5, 5)] = jnp.zeros((5,) + store.shape[1:], BF)
+        nothing = empty[...].astype(BF)
+        for sub in range(5):
+            for side in range(2):
+                store[index * 5 + sub, side] = nothing
         return carry
 
     lax.fori_loop(0, slots // 5, clear, 0)
@@ -292,7 +296,7 @@
         both = jnp.dot(features[e, :, 0:48], mine[t], preferred_element_type=F32)
         partner_width = jnp.broadcast_to(param[e, 4:5, :], (128, 128)).T
         widths = partner_width + param[place_of(t), 4:5, :]
-        coulomb = lax.rsqrt(both[:, 128:])
+        coulomb = lax.rsqrt(both[:, 128:].astype(BF))
         response = RESPONSE_SCALE * jnp.exp2(both[:, :128] / widths)
         if masked:
             same = lax.broadcasted_iota(jnp.int32, (128, 128), 0) == lax.broadcasted_iota(
@@ -562,6 +566,7 @@
         scratch_shapes=[
             pltpu.VMEM((nx, ny, nz, 8, lanes), F32),
             pltpu.VMEM((nx, ny, nz, 1, lanes), F32),
+            pltpu.VMEM((lanes, lanes), F32),
             pltpu.VMEM(positions.shape, F32),
             pltpu.VMEM(shield.shape, F32),
             pltpu.VMEM(width.shape, F32),

time: 81.6 us -> 80.9 us (level)
    pallas_call x1, Pallas kernels: 44.9 us -> 48.3 us  [on_device(): pl.pallas_call(solve, out_shape=(shape, shape), in_specs=[VMEM_SPEC] * 8,...]
    pallas_call x1, Pallas kernels: 14.2 us -> 11.3 us  [on_device(): pl.pallas_call(first_halo, out_shape=(pltpu.VMEM(ext + (8, lanes), F32),...]
where the time goes in v6:
time: 80.9 us; the launch traced here: 81.2 us
  Pallas kernels  79.3 us (98%)
  local copies, waits for them, and re-layouts  1.26 us (2%)
    pallas_call x1, Pallas kernels, on_device(): pl.pallas_call(solve, out_shape=(shape, shape), in_specs=[VMEM_SPEC] * 8,...  48.3 us
    pallas_call x1, Pallas kernels, on_device(): pl.pallas_call(build, out_shape=(pltpu.VMEM(blank.shape, BF),) + (pltpu.V...  19.7 us
    pallas_call x1, Pallas kernels, on_device(): pl.pallas_call(first_halo, out_shape=(pltpu.VMEM(ext + (8, lanes), F32),...  11.3 us

profile of v6, /device:TPU:1, one launch (start us, length us, event | category | flops | bytes accessed | tf_op | source)
XLA Modules:
  0.0 81.2 jit_solution(10737008527953872669)
XLA Ops:
  0.6 11.3 %first_halo.1 = (f32[4,4,10,8,128]{4,3,2,1,0:T(8,128)S(1)}, f32[4,4,10,1,128]{4,3,2,1,0:T(1,128)S(1)}, bf16[865,2,128,128]{3,2,1,0:T(8,128)(2,1)S(1)}) custom-call(f32[3,2,2,8,128]{4,3,2,1,0:T(8,128)} %pos_in.1, f32[2,2,8,128]{3,2,1,0:T(8,128)} %shield_in.1, f32[2,2,8,128]{3,2,1,0:T(8,128)} %width_in.1, f32[4,2,2,8,128]{4,3,2,1,0:T(8,128)} %rhs_in.1), custom_call_target="tpu_custom_call" | custom-call | tf_op jit(solution)/shard_map/first_halo/pallas_call | solution.py:557
  11.9 19.7 %build.1 = (bf16[865,2,128,128]{3,2,1,0:T(8,128)(2,1)S(1)}, f32[32,4,128]{2,1,0:T(4,128)S(1)}, f32[32,4,128]{2,1,0:T(4,128)S(1)}, f32[32,4,128]{2,1,0:T(4,128)S(1)}, f32[32,4,128]{2,1,0:T(4,128)S(1)}) custom-call(s32[2,2,8]{2,1,0:T(2,128)} %bits.1, f32[160,8,128]{2,1,0:T(8,128)S(1)} %bitcast.10, ...), custom_call_target="tpu_custom_call", output_to_operand_aliasing={{0}: (6, {})} | custom-call | tf_op jit(solution)/shard_map/build/pallas_call | solution.py:583
  31.6 48.3 %solve.1 = (f32[4,4,8,128]{3,2,1,0:T(8,128)S(1)}, f32[4,4,8,128]{3,2,1,0:T(8,128)S(1)}) custom-call(f32[32,4,128]{2,1,0:T(4,128)S(1)} %get-tuple-element.15.u0, f32[2,2,8,4,128]{4,3,2,1,0:T(4,128)S(1)} %bitcast.14, f32[32,4,128]{2,1,0:T(4,128)S(1)} %get-tuple-element.17.w0, f32[32,4,128]{2,1,0:T(4,128)S(1)} %get-tuple-element.18.diagonal, ...), custom_call_target="tpu_custom_call" | custom-call | tf_op jit(solution)/shard_map/solve/pallas_call | solution.py:612
  79.9 0.6 copy.14
  80.6 0.6 copy.15
